TPU v7x, 32 devices: a whole 2x2x4 slice. The times are simulated.
32 devices in a mesh: slab: 8 (over y, x, core), cross: 4 (over z).
Axes of the slice: x: 2, y: 2, z: 4, core: 2. Of those that a mesh axis runs over, the one named last changes fastest.
Arguments:
- populations: float32 [19, 32, 32, 128], P(None, 'slab', 'cross'), may hold values from 0 to 1, as said below
- fluid_mask: int32 [32, 32, 128], P('slab', 'cross'), may hold values 0 or 1
- relaxation: float32 [32, 32, 128], P('slab', 'cross'), may hold values from 0.8 to 1.7
- positions: int32 [3, 128, 642], P(None, 'slab'), may hold values from -1 to 127, as said below
- triangles: int32 [3, 1280], replicated, may hold values from 0 to 641, as said below
- tension: float32 [128, 1280], P('slab'), may hold values from 0.0003 to 0.003
- coarse_moments: float32 [4, 4096], P(None, 'slab'), may hold values from -0.2 to 1.2, as said below
- interface: int32 [3, 4096], P(None, ('slab', 'cross')), may hold values from -1 to 4095, as said below
Outputs:
- populations_next: float32 [19, 32, 32, 128], P(None, 'slab', 'cross')
- flow: float32 [3, 32, 32, 128], P(None, 'slab', 'cross')
Inputs may be any that keep to these rules, and one draw needn't show every extreme that they name: `positions`: nodes of membrane m lie in planes 4 * (m // 16) - 1 to 4 * (m // 16) + 4, columns 0 to 31 and rows 0 to 127. `triangles`: each triangle names three different nodes of a membrane. `interface`: in each block of 128 columns (one device's, slab major), row 0 names different cells of that device's block, numbered (plane * 8 + column) * 128 + row, or -1 for an unused slot; rows 1 and 2 name coarse cells. `populations`: populations are positive. `coarse_moments`: row 0 is a positive density, rows 1 to 3 a velocity.
All inputs are finite; a program needn't handle non-finite values. No bound on the sum of `fluid_mask` on one device may be relied on, other than what follows from the above.
Results may differ from a plain program's by a relative error of at most 0.0001.
Values sent between devices are 32-bit elements; how exact they have to be, the bound alone decides.
A program may use at most 128 MiB of HBM per device.

v0:
```python
import functools
import math

import jax
import jax.numpy as jnp
from jax import lax
from jax.experimental import pallas as pl
from jax.experimental.pallas import tpu as pltpu
from jax.sharding import PartitionSpec as P

STEPS = 4
MESH = pl.DeviceIdType.MESH
LATTICE_VECTORS = [
    (0, 0, 0),
    (1, 0, 0),
    (-1, 0, 0),
    (0, 1, 0),
    (0, -1, 0),
    (0, 0, 1),
    (0, 0, -1),
    (1, 1, 0),
    (-1, -1, 0),
    (1, -1, 0),
    (-1, 1, 0),
    (1, 0, 1),
    (-1, 0, -1),
    (1, 0, -1),
    (-1, 0, 1),
    (0, 1, 1),
    (0, -1, -1),
    (0, 1, -1),
    (0, -1, 1),
]
LATTICE_WEIGHTS = [1.0 / 3.0] + [1.0 / 18.0] * 6 + [1.0 / 36.0] * 12
OPPOSITE = [0] + [q + 1 if q % 2 == 1 else q - 1 for q in range(1, 19)]
ROOT_THREE = math.sqrt(3.0)
DIRECTIONS = [(1, 0), (-1, 0), (0, 1), (0, -1), (1, 1), (-1, -1), (1, -1), (-1, 1)]
NT = (((1,), (1,)), ((), ()))
F32, BF16, I32 = jnp.float32, jnp.bfloat16, jnp.int32


def round_up(value, unit):
    return (value + unit - 1) // unit * unit


def split(value, parts):
    pieces = []
    for _ in range(parts):
        piece = value.astype(BF16).astype(F32)
        pieces.append(piece)
        value = value - piece
    return pieces


def nodal_stage(plane_count, columns, rows, pos_ref, tri_ref, ten_ref, xs, inc, force):
    dims, membranes, nodes = pos_ref.shape
    padded = xs.shape[2]
    triangles = tri_ref.shape[1]
    slab = lax.axis_index("slab")
    cross = lax.axis_index("cross")

    xs[...] = jnp.zeros_like(xs)
    xs[0, :, :nodes] = (pos_ref[0] - slab * plane_count).astype(F32)
    xs[1, :, :nodes] = (pos_ref[1] - cross * columns).astype(F32)
    xs[2, :, :nodes] = (pos_ref[2] - rows // 2).astype(F32)

    corners = [tri_ref[pl.ds(corner, 1), :] for corner in range(3)]
    chunk = 128

    @pl.loop(0, padded // chunk)
    def _(i):
        ids = lax.broadcasted_iota(I32, (chunk, triangles), 0) + i * chunk
        hit = (ids == corners[0]) | (ids == corners[1]) | (ids == corners[2])
        inc[pl.ds(pl.multiple_of(i * chunk, chunk), chunk), :] = jnp.where(hit, 1.0, 0.0).astype(BF16)

    coords = xs[...].reshape(dims * membranes, padded)
    sums = jnp.dot(coords.astype(BF16), inc[...], preferred_element_type=F32)
    tension = ten_ref[...]
    terms = jnp.concatenate(
        [sums[k * membranes : (k + 1) * membranes] * tension for k in range(3)] + [tension], axis=0
    )
    stacked = jnp.concatenate(split(terms, 3), axis=0).astype(BF16)
    gathered = lax.dot_general(stacked, inc[...], NT, preferred_element_type=F32)
    count = terms.shape[0]
    total = gathered[:count] + (gathered[count : 2 * count] + gathered[2 * count :])
    weight = total[3 * membranes :]
    for k in range(3):
        force[k] = total[k * membranes : (k + 1) * membranes] - 3.0 * xs[k] * weight


def spread_stage(xs, force, acc, out_ref):
    _, membranes, padded = xs.shape
    _, planes, columns, rows = out_ref.shape
    plane_count = planes - 4
    half = (columns + 2) // 2
    cells = acc.shape[0] // 6
    acc[...] = jnp.zeros_like(acc)
    unroll = 4 if membranes % 4 == 0 else 1

    @pl.loop(0, membranes // unroll)
    def _(i):
        running = None
        for inner in range(unroll):
            m = pl.ds(i * unroll + inner, 1)
            plane = xs[0, m, :].astype(I32) + 1
            column = xs[1, m, :].astype(I32) + 1
            row = xs[2, m, :].astype(I32) + rows // 2
            inside = (column >= 0) & (column < 2 * half)
            upper = column >= half
            cell = plane * half + jnp.where(upper, column - half, column)
            cell = jnp.where(inside, cell, -1)
            lane = row + jnp.where(upper, rows, 0)
            mask = lax.broadcasted_iota(I32, (cells, padded), 0) == cell
            values = [split(force[k, m, :], 2) for k in range(3)]
            left = jnp.concatenate(
                [jnp.where(mask, values[k][part], 0.0) for part in range(2) for k in range(3)], axis=0
            ).astype(BF16)
            right = jnp.where(
                lax.broadcasted_iota(I32, (2 * rows, padded), 0) == lane, 1.0, 0.0
            ).astype(BF16)
            product = lax.dot_general(left, right, NT, preferred_element_type=F32)
            running = product if running is None else running + product
        acc[...] += running

    for k in range(3):
        value = acc[k * cells : (k + 1) * cells] + acc[(3 + k) * cells : (4 + k) * cells]
        halves = []
        for part in range(2):
            b = value[:, part * rows : (part + 1) * rows]
            halves.append(0.5 * b + 0.25 * (pltpu.roll(b, 1, 1) + pltpu.roll(b, rows - 1, 1)))
        smooth = []
        for p in range(plane_count + 2):
            b = jnp.concatenate([h[p * half : (p + 1) * half] for h in halves], axis=0)
            smooth.append(
                0.5 * b[1 : columns + 1] + 0.25 * (b[:columns] + b[2 : columns + 2])
            )
        for j in range(planes):
            total_plane = jnp.zeros((columns, rows), F32)
            for source, w in ((j - 2, 0.25), (j - 1, 0.5), (j, 0.25)):
                if 0 <= source < plane_count + 2:
                    total_plane = total_plane + w * smooth[source]
            out_ref[k, j] = total_plane


def equilibrium_pairs(density, velocity):
    squared = velocity[0] * velocity[0] + velocity[1] * velocity[1] + velocity[2] * velocity[2]
    base = 1.0 - 1.5 * squared
    result = [None] * 19
    result[0] = LATTICE_WEIGHTS[0] * density * base
    scaled = {w: w * density for w in (1.0 / 18.0, 1.0 / 36.0)}
    for q in range(1, 19, 2):
        projected = None
        for c, v in zip(LATTICE_VECTORS[q], velocity):
            if c == 0:
                continue
            if projected is None:
                projected = v if c == 1 else -v
            else:
                projected = projected + v if c == 1 else projected - v
        even = base + 4.5 * projected * projected
        odd = 3.0 * projected
        weight = scaled[LATTICE_WEIGHTS[q]]
        result[q] = weight * (even + odd)
        result[q + 1] = weight * (even - odd)
    return result


def moments_of(fields):
    density = functools.reduce(lambda a, b: a + b, fields)
    momentum = []
    for k in range(3):
        plus = [fields[q] for q in range(19) if LATTICE_VECTORS[q][k] == 1]
        minus = [fields[q] for q in range(19) if LATTICE_VECTORS[q][k] == -1]
        momentum.append(functools.reduce(lambda a, b: a + b, [a - b for a, b in zip(plus, minus)]))
    return density, momentum


def moving(dim, sign):
    return [q for q in range(19) if LATTICE_VECTORS[q][dim] == sign]


def lattice_kernel(
    slabs, crosses,
    tri_hbm, pos_hbm, ten_hbm, coarse_hbm, face_hbm, relax_hbm, fluid_hbm, pop_hbm,
    next_ref,
    tri_ref, pos_ref, ten_ref, coarse_ref, face_ref, relax_ref, fluid_ref, pop_ref,
    xs, inc, nodal, acc, force_ref,
    relaxed, pushed, rim, used_ref, coarse_all, parts,
    force_in, zsend, zrecv, xsend, xrecv, csend, crecv,
    load_sems, coarse_sems, force_sems, send_sems, recv_sems,
):
    _, plane_count, columns, rows = pop_ref.shape
    slab = lax.axis_index("slab")
    cross = lax.axis_index("cross")

    def beside(direction, sign):
        dz, dx = direction[0] * sign, direction[1] * sign
        conditions = []
        if dz == 1:
            conditions.append(slab < slabs - 1)
        if dz == -1:
            conditions.append(slab > 0)
        if dx == 1:
            conditions.append(cross < crosses - 1)
        if dx == -1:
            conditions.append(cross > 0)
        return functools.reduce(jnp.logical_and, conditions)

    def target(direction):
        return {"slab": slab + direction[0], "cross": cross + direction[1]}

    loads = [
        pltpu.make_async_copy(source, sink, load_sems.at[i])
        for i, (source, sink) in enumerate(
            (
                (tri_hbm, tri_ref),
                (pos_hbm, pos_ref),
                (ten_hbm, ten_ref),
                (coarse_hbm, coarse_ref),
                (face_hbm, face_ref),
                (relax_hbm, relax_ref),
                (fluid_hbm, fluid_ref),
                (pop_hbm, pop_ref),
            )
        )
    ]
    for load in loads:
        load.start()

    force_in[...] = jnp.zeros_like(force_in)
    zrecv[...] = jnp.zeros_like(zrecv)
    xrecv[...] = jnp.zeros_like(xrecv)
    crecv[...] = jnp.zeros_like(crecv)
    parts[...] = jnp.zeros_like(parts)

    barrier = pltpu.get_barrier_semaphore()

    @pl.loop(1, slabs)
    def _(d):
        peer = lax.rem(slab + d, slabs)
        pl.semaphore_signal(
            barrier, inc=1, device_id={"slab": peer, "cross": cross}, device_id_type=MESH
        )

    expected = slabs - 1
    for direction in DIRECTIONS:
        if direction[1] == 0:
            continue
        there = beside(direction, 1)
        expected = expected + jnp.where(there, 1, 0)

        @pl.when(there)
        def _():
            pl.semaphore_signal(
                barrier, inc=1, device_id=target(direction), device_id_type=MESH
            )

    for load in loads[:3]:
        load.wait()
    nodal_stage(plane_count, columns, rows, pos_ref, tri_ref, ten_ref, xs, inc, nodal)
    loads[3].wait()
    pl.semaphore_wait(barrier, expected)
    coarse_all[slab] = coarse_ref[...]

    def coarse_copy(d):
        return pltpu.make_async_remote_copy(
            src_ref=coarse_ref,
            dst_ref=coarse_all.at[slab],
            send_sem=coarse_sems.at[0, d],
            recv_sem=coarse_sems.at[1, d],
            device_id={"slab": lax.rem(slab + d, slabs), "cross": cross},
            device_id_type=MESH,
        )

    @pl.loop(1, slabs)
    def _(d):
        coarse_copy(d).start()

    spread_stage(xs, nodal, acc, force_ref)

    def force_copy(index):
        start = plane_count + 2 if index == 0 else 0
        return pltpu.make_async_remote_copy(
            src_ref=force_ref.at[:, pl.ds(start, 2)],
            dst_ref=force_in.at[index],
            send_sem=force_sems.at[0, index],
            recv_sem=force_sems.at[1, index],
            device_id=target(DIRECTIONS[index]),
            device_id_type=MESH,
        )

    for index in range(2):

        @pl.when(beside(DIRECTIONS[index], 1))
        def _():
            force_copy(index).start()

    for load in loads[4:]:
        load.wait()

    cell = face_ref[pl.ds(0, 1), :]
    slots = cell.shape[1]
    used = cell >= 0
    place = jnp.where(used, cell // rows, -1)
    lane = jnp.where(used, cell % rows, -1)
    first = face_ref[pl.ds(1, 1), :]
    second = face_ref[pl.ds(2, 1), :]
    width = coarse_ref.shape[1]

    @pl.loop(1, slabs)
    def _(d):
        pltpu.make_async_remote_copy(
            src_ref=coarse_ref,
            dst_ref=coarse_all.at[lax.rem(slab + slabs - d, slabs)],
            send_sem=coarse_sems.at[0, d],
            recv_sem=coarse_sems.at[1, d],
            device_id={"slab": lax.rem(slab + d, slabs), "cross": cross},
            device_id_type=MESH,
        ).wait_recv()

    def blend(j, running):
        for i, piece in enumerate(split(coarse_all[j], 3)):
            parts[pl.ds(8 * i, 4), :] = piece
        ids = lax.broadcasted_iota(I32, (width, slots), 0) + j * width
        table = jnp.where(ids == first, 0.75, 0.0) + jnp.where(ids == second, 0.25, 0.0)
        return running + jnp.dot(
            parts[...].astype(BF16), table.astype(BF16), preferred_element_type=F32
        )

    mixed = lax.fori_loop(0, slabs, blend, jnp.zeros((24, slots), F32))
    blended = mixed[0:4] + (mixed[8:12] + mixed[16:20])

    cells = plane_count * columns
    mask = lax.broadcasted_iota(I32, (cells, slots), 0) == place
    pieces = split(blended, 3)
    left = [jnp.where(mask, piece[m : m + 1], 0.0) for m in range(4) for piece in pieces]
    left.append(jnp.where(mask, 1.0, 0.0))
    right = jnp.where(lax.broadcasted_iota(I32, (rows, slots), 0) == lane, 1.0, 0.0)
    placed = lax.dot_general(
        jnp.concatenate(left, axis=0).astype(BF16), right.astype(BF16), NT, preferred_element_type=F32
    )

    def placed_at(index, p):
        start = index * cells + p * columns
        return placed[start : start + columns]

    for p in range(plane_count):
        filled = [
            placed_at(3 * m, p) + (placed_at(3 * m + 1, p) + placed_at(3 * m + 2, p)) for m in range(4)
        ]
        used_ref[p] = placed_at(12, p)
        for q, value in enumerate(equilibrium_pairs(filled[0], filled[1:])):
            rim[q, p] = value

    for index in range(2):

        @pl.when(beside(DIRECTIONS[index], -1))
        def _():
            force_copy(index).wait_recv()

    for k in range(3):
        for p in range(plane_count):
            value = force_ref[k, p + 2]
            if p < 2:
                value = value + force_in[0, k, p]
            if p >= plane_count - 2:
                value = value + force_in[1, k, p - plane_count + 2]
            pushed[k, p] = value / relax_ref[p]

    sublane = lax.broadcasted_iota(I32, (columns, rows), 0)
    ups, downs = moving(0, 1), moving(0, -1)
    rights, lefts = moving(1, 1), moving(1, -1)
    corner_of = {7: 0, 8: 1, 9: 2, 10: 3}

    def halo_copy(step, index):
        if index < 2:
            source, sink = zsend.at[step, index], zrecv.at[step, index]
        elif index < 4:
            source, sink = xsend.at[step, index - 2], xrecv.at[step, index - 2]
        else:
            source, sink = csend.at[step, index - 4], crecv.at[step, index - 4]
        return pltpu.make_async_remote_copy(
            src_ref=source,
            dst_ref=sink,
            send_sem=send_sems.at[step % 2, index],
            recv_sem=recv_sems.at[step % 2, index],
            device_id=target(DIRECTIONS[index]),
            device_id_type=MESH,
        )

    for step in range(STEPS):
        fields_ref = pop_ref if step == 0 else next_ref
        for p in range(plane_count):
            fields = [fields_ref[q, p] for q in range(19)]
            density, momentum = moments_of(fields)
            inverse = 1.0 / density
            shifted = [(momentum[k] + pushed[k, p]) * inverse for k in range(3)]
            rate = relax_ref[p]
            fluid = fluid_ref[p] == 1
            for q, goal in enumerate(equilibrium_pairs(density, shifted)):
                value = fields[q] + rate * (goal - fields[q])
                value = jnp.where(fluid, value, fields[OPPOSITE[q]])
                relaxed[q, p] = value
                if p == plane_count - 1 and q in ups:
                    zsend[step, 0, ups.index(q)] = value
                if p == 0 and q in downs:
                    zsend[step, 1, downs.index(q)] = value
                if q in rights:
                    xsend[step, 0, rights.index(q), p : p + 1] = value[columns - 1 :]
                if q in lefts:
                    xsend[step, 1, lefts.index(q), p : p + 1] = value[:1]
                if q in corner_of:
                    cz, cx, _ = LATTICE_VECTORS[q]
                    if p == (plane_count - 1 if cz == 1 else 0):
                        edge = value[columns - 1 :] if cx == 1 else value[:1]
                        csend[step, corner_of[q]] = edge
        for index in (4, 5, 6, 7, 0, 1, 2, 3):

            @pl.when(beside(DIRECTIONS[index], 1))
            def _():
                if step >= 2:
                    halo_copy(step - 2, index).wait_send()
                halo_copy(step, index).start()

        for index in range(8):

            @pl.when(beside(DIRECTIONS[index], -1))
            def _():
                halo_copy(step, index).wait_recv()

        for p in range(plane_count):
            fixed = used_ref[p] > 0.5
            for q, (cz, cx, cy) in enumerate(LATTICE_VECTORS):
                source = p - cz
                within = 0 <= source < plane_count
                if within:
                    value = relaxed[q, source]
                elif cz == 1:
                    value = zrecv[step, 0, ups.index(q)]
                else:
                    value = zrecv[step, 1, downs.index(q)]
                if cx != 0:
                    side, members = (0, rights) if cx == 1 else (1, lefts)
                    if within:
                        edge = xrecv[step, side, members.index(q), source : source + 1]
                    else:
                        edge = crecv[step, corner_of[q]]
                    value = pltpu.roll(value, cx % columns, 0)
                    at = 0 if cx == 1 else columns - 1
                    value = jnp.where(sublane == at, edge, value)
                if cy != 0:
                    value = pltpu.roll(value, cy % rows, 1)
                next_ref[q, p] = jnp.where(fixed, rim[q, p], value)

    @pl.loop(1, slabs)
    def _(d):
        coarse_copy(d).wait_send()

    for index in range(2):

        @pl.when(beside(DIRECTIONS[index], 1))
        def _():
            force_copy(index).wait_send()

    for index in range(8):

        @pl.when(beside(DIRECTIONS[index], 1))
        def _():
            for step in range(max(0, STEPS - 2), STEPS):
                halo_copy(step, index).wait_send()


def flow_kernel(fields_ref, next_ref, flow_ref):
    for p in range(fields_ref.shape[1]):
        fields = [fields_ref[q, p] for q in range(19)]
        for q, value in enumerate(fields):
            next_ref[q, p] = value
        density, momentum = moments_of(fields)
        inverse = ROOT_THREE / density
        for k in range(3):
            flow_ref[k, p] = momentum[k] * inverse


def on_device(
    slabs, crosses,
    populations, fluid_mask, relaxation, positions, triangles, tension, coarse_moments, interface,
):
    _, plane_count, columns, rows = populations.shape
    _, membranes, nodes = positions.shape
    padded = round_up(nodes, 128)
    corners = triangles.shape[1]
    half = (columns + 2) // 2
    cells = round_up((plane_count + 2) * half, 16)
    vmem = pl.BlockSpec(memory_space=pltpu.VMEM)
    block = (19, plane_count, columns, rows)
    operands = (
        triangles, positions, tension, coarse_moments, interface, relaxation, fluid_mask, populations,
    )
    fields = pl.pallas_call(
        functools.partial(lattice_kernel, slabs, crosses),
        name="lattice_steps",
        out_shape=jax.ShapeDtypeStruct(block, F32),
        in_specs=[pl.BlockSpec(memory_space=pl.ANY)] * 8,
        out_specs=vmem,
        scratch_shapes=[pltpu.VMEM(operand.shape, operand.dtype) for operand in operands]
        + [
            pltpu.VMEM((3, membranes, padded), F32),
            pltpu.VMEM((padded, corners), BF16),
            pltpu.VMEM((3, membranes, padded), F32),
            pltpu.VMEM((6 * cells, 2 * rows), F32),
            pltpu.VMEM((3, plane_count + 4, columns, rows), F32),
            pltpu.VMEM(block, F32),
            pltpu.VMEM((3,) + block[1:], F32),
            pltpu.VMEM(block, F32),
            pltpu.VMEM(block[1:], F32),
            pltpu.VMEM((slabs,) + coarse_moments.shape, F32),
            pltpu.VMEM((24, coarse_moments.shape[1]), F32),
            pltpu.VMEM((2, 3, 2, columns, rows), F32),
            pltpu.VMEM((STEPS, 2, 5, columns, rows), F32),
            pltpu.VMEM((STEPS, 2, 5, columns, rows), F32),
            pltpu.VMEM((STEPS, 2, 5, plane_count, rows), F32),
            pltpu.VMEM((STEPS, 2, 5, plane_count, rows), F32),
            pltpu.VMEM((STEPS, 4, 1, rows), F32),
            pltpu.VMEM((STEPS, 4, 1, rows), F32),
            pltpu.SemaphoreType.DMA((8,)),
            pltpu.SemaphoreType.DMA((2, slabs)),
            pltpu.SemaphoreType.DMA((2, 2)),
            pltpu.SemaphoreType.DMA((2, 8)),
            pltpu.SemaphoreType.DMA((2, 8)),
        ],
        compiler_params=pltpu.CompilerParams(collective_id=0, has_side_effects=True),
    )(*operands)
    return pl.pallas_call(
        flow_kernel,
        name="flow",
        out_shape=(
            jax.ShapeDtypeStruct(block, F32),
            jax.ShapeDtypeStruct((3,) + block[1:], F32),
        ),
        in_specs=[vmem],
        out_specs=(vmem, vmem),
    )(fields)


def solution(mesh):
    in_specs = (
        P(None, "slab", "cross", None),
        P("slab", "cross", None),
        P("slab", "cross", None),
        P(None, "slab", None),
        P(),
        P("slab", None),
        P(None, "slab"),
        P(None, ("slab", "cross")),
    )
    out_specs = (P(None, "slab", "cross", None), P(None, "slab", "cross", None))
    return jax.shard_map(
        functools.partial(on_device, mesh.shape["slab"], mesh.shape["cross"]),
        mesh=mesh, in_specs=in_specs, out_specs=out_specs, check_vma=False,
    )
```

profile of v0, /device:TPU:11, one launch (start us, length us, event | category | flops | bytes accessed | tf_op | source)
XLA Modules:
  0.0 27.4 jit_solution(16625904284592087414)
XLA Ops:
  0.6 25.0 %lattice_steps.1.fields_ref = f32[19,4,8,128]{3,2,1,0:T(8,128)} custom-call(s32[3,1280]{1,0:T(4,128)} %tri_hbm.1, s32[3,16,642]{2,1,0:T(8,128)} %pos_hbm.1, f32[16,1280]{1,0:T(8,128)} %ten_hbm.1, f32[4,512]{1,0:T(4,128)} %coarse_hbm.1, s32[3,128]{1,0:T(4,128)} %face_hbm.1, f32[4,8,128]{2,1,0:T(8,128)} %relax_hbm.1, s32[4,8,128]{2,1,0:T(8,128)} %fluid_hbm.1, ...), custom_call_target="tpu_custom_call" | custom-call | tf_op jit(solution)/shard_map/lattice_steps/pallas_call | solution.py:499
  25.6 1.7 %flow.1 = (f32[19,4,8,128]{3,2,1,0:T(8,128)}, f32[3,4,8,128]{3,2,1,0:T(8,128)}) custom-call(f32[19,4,8,128]{3,2,1,0:T(8,128)} %lattice_steps.1.fields_ref), custom_call_target="tpu_custom_call" | custom-call | tf_op jit(solution)/shard_map/flow/pallas_call | solution.py:533
where the time goes:
time: 27.9 us; the launch traced here: 27.4 us
  Pallas kernels  26.7 us (96%)
  between operations  0.64 us (2%)
    pallas_call x1, Pallas kernels, on_device(): pl.pallas_call(functools.partial(lattice_kernel, slabs, crosses), name='l...  25 us
    pallas_call x1, Pallas kernels, on_device(): pl.pallas_call(flow_kernel, name='flow', out_shape=(jax.ShapeDtypeStruct(...  1.72 us

commit v1 on v0

--- a/solution.py
+++ b/solution.py
@@ -470,15 +470,19 @@
                 halo_copy(step, index).wait_send()
 
 
-def flow_kernel(fields_ref, next_ref, flow_ref):
+def flow_kernel(fields_ref, next_ref, flow_ref, flow, sems):
+    whole = pltpu.make_async_copy(fields_ref, next_ref, sems.at[0])
+    whole.start()
     for p in range(fields_ref.shape[1]):
         fields = [fields_ref[q, p] for q in range(19)]
-        for q, value in enumerate(fields):
-            next_ref[q, p] = value
         density, momentum = moments_of(fields)
         inverse = ROOT_THREE / density
         for k in range(3):
-            flow_ref[k, p] = momentum[k] * inverse
+            flow[k, p] = momentum[k] * inverse
+    part = pltpu.make_async_copy(flow, flow_ref, sems.at[1])
+    part.start()
+    whole.wait()
+    part.wait()
 
 
 def on_device(
@@ -499,7 +503,7 @@
     fields = pl.pallas_call(
         functools.partial(lattice_kernel, slabs, crosses),
         name="lattice_steps",
-        out_shape=jax.ShapeDtypeStruct(block, F32),
+        out_shape=pltpu.VMEM(block, F32),
         in_specs=[pl.BlockSpec(memory_space=pl.ANY)] * 8,
         out_specs=vmem,
         scratch_shapes=[pltpu.VMEM(operand.shape, operand.dtype) for operand in operands]
@@ -538,8 +542,9 @@
             jax.ShapeDtypeStruct((3,) + block[1:], F32),
         ),
         in_specs=[vmem],
-        out_specs=(vmem, vmem),
-    )(fields)
+        out_specs=(pl.BlockSpec(memory_space=pl.ANY),) * 2,
+        scratch_shapes=[pltpu.VMEM((3,) + block[1:], F32), pltpu.SemaphoreType.DMA((2,))],
+    )(pltpu.with_memory_space_constraint(fields, pltpu.VMEM))
 
 
 def solution(mesh):

time: 27.9 us -> 26.2 us (0.939)
  Pallas kernels: 26.7 us -> 25 us
    pallas_call x1, Pallas kernels: 1.72 us -> 0.74 us  [on_device(): pl.pallas_call(flow_kernel, name='flow', out_shape=(jax.ShapeDtypeStruct(...]
    pallas_call x1, Pallas kernels: 25 us -> 24.3 us  [on_device(): pl.pallas_call(functools.partial(lattice_kernel, slabs, crosses), name='l...]
where the time goes in v1:
time: 26.2 us; the launch traced here: 25.7 us
  Pallas kernels  25 us (95%)
  between operations  0.64 us (2%)
    pallas_call x1, Pallas kernels, on_device(): pl.pallas_call(functools.partial(lattice_kernel, slabs, crosses), name='l...  24.3 us
    pallas_call x1, Pallas kernels, on_device(): pl.pallas_call(flow_kernel, name='flow', out_shape=(jax.ShapeDtypeStruct(...  0.74 us

profile of v1, /device:TPU:11, one launch (start us, length us, event | category | flops | bytes accessed | tf_op | source)
XLA Modules:
  0.0 25.7 jit_solution(1334710690512087127)
XLA Ops:
  0.6 24.3 %lattice_steps.1.fields_ref = f32[19,4,8,128]{3,2,1,0:T(8,128)S(1)} custom-call(s32[3,1280]{1,0:T(4,128)} %tri_hbm.1, s32[3,16,642]{2,1,0:T(8,128)} %pos_hbm.1, f32[16,1280]{1,0:T(8,128)} %ten_hbm.1, f32[4,512]{1,0:T(4,128)} %coarse_hbm.1, s32[3,128]{1,0:T(4,128)} %face_hbm.1, f32[4,8,128]{2,1,0:T(8,128)} %relax_hbm.1, s32[4,8,128]{2,1,0:T(8,128)} %fluid_hbm.1, ...), custom_call_target="tpu_custom_call" | custom-call | tf_op jit(solution)/shard_map/lattice_steps/pallas_call | solution.py:503
  24.9 0.7 %flow.1 = (f32[19,4,8,128]{3,2,1,0:T(8,128)}, f32[3,4,8,128]{3,2,1,0:T(8,128)}) custom-call(f32[19,4,8,128]{3,2,1,0:T(8,128)S(1)} %lattice_steps.1.fields_ref), custom_call_target="tpu_custom_call" | custom-call | tf_op jit(solution)/shard_map/flow/pallas_call | solution.py:537

commit v2 on v1

v2 whole, which is shorter than its diff:
```python
import functools
import math

import jax
import jax.numpy as jnp
from jax import lax
from jax.experimental import pallas as pl
from jax.experimental.pallas import tpu as pltpu
from jax.sharding import PartitionSpec as P

STEPS = 4
MESH = pl.DeviceIdType.MESH
LATTICE_VECTORS = [
    (0, 0, 0),
    (1, 0, 0),
    (-1, 0, 0),
    (0, 1, 0),
    (0, -1, 0),
    (0, 0, 1),
    (0, 0, -1),
    (1, 1, 0),
    (-1, -1, 0),
    (1, -1, 0),
    (-1, 1, 0),
    (1, 0, 1),
    (-1, 0, -1),
    (1, 0, -1),
    (-1, 0, 1),
    (0, 1, 1),
    (0, -1, -1),
    (0, 1, -1),
    (0, -1, 1),
]
LATTICE_WEIGHTS = [1.0 / 3.0] + [1.0 / 18.0] * 6 + [1.0 / 36.0] * 12
OPPOSITE = [0] + [q + 1 if q % 2 == 1 else q - 1 for q in range(1, 19)]
ROOT_THREE = math.sqrt(3.0)
DIRECTIONS = [(1, 0), (-1, 0), (0, 1), (0, -1), (1, 1), (-1, -1), (1, -1), (-1, 1)]
NT = (((1,), (1,)), ((), ()))
F32, BF16, I32, I16 = jnp.float32, jnp.bfloat16, jnp.int32, jnp.int16
HALO = 2
SLAB_MOVES = [
    [(q, depth) for depth in (1, 2) for q in range(19) if LATTICE_VECTORS[q][0] * sign >= depth - 1]
    for sign in (1, -1)
]
CROSS_MOVES = [
    [(q, depth) for depth in (1, 2) for q in range(19) if LATTICE_VECTORS[q][1] * sign >= depth - 1]
    for sign in (1, -1)
]
CORNER_MOVES = [
    [
        (q, dz, dx)
        for dz in (1, 2)
        for dx in (1, 2)
        for q in range(19)
        if LATTICE_VECTORS[q][0] * sz >= dz - 1 and LATTICE_VECTORS[q][1] * sx >= dx - 1
    ]
    for sz, sx in DIRECTIONS[4:]
]


def round_up(value, unit):
    return (value + unit - 1) // unit * unit


def split(value, parts):
    pieces = []
    for _ in range(parts):
        piece = value.astype(BF16).astype(F32)
        pieces.append(piece)
        value = value - piece
    return pieces


def incidence_stage(tri_ref, inc, nodes):
    triangles = tri_ref.shape[1]
    tiles = triangles // 128
    corners = [
        [
            jnp.broadcast_to(tri_ref[pl.ds(k, 1), t * 128 : (t + 1) * 128], (16, 128)).astype(I16)
            for t in range(tiles)
        ]
        for k in range(3)
    ]
    iota = lax.broadcasted_iota(I32, (16, 128), 0)

    def rows_at(start):
        ids = (iota + start).astype(I16)
        for t in range(tiles):
            hit = (ids == corners[0][t]) | (ids == corners[1][t]) | (ids == corners[2][t])
            inc[pl.ds(start, 16), t * 128 : (t + 1) * 128] = jnp.where(
                hit, jnp.ones((), BF16), jnp.zeros((), BF16)
            )

    chunk = 128

    @pl.loop(0, nodes // chunk)
    def _(i):
        for r in range(chunk // 16):
            rows_at(pl.multiple_of(i * chunk + r * 16, 16))

    done = nodes // chunk * chunk
    while done < nodes:
        rows_at(done)
        done += 16
    if done < inc.shape[0]:
        inc[done:, :] = jnp.zeros((inc.shape[0] - done, triangles), BF16)


def nodal_stage(plane_count, columns, rows, pos_ref, ten_ref, inc, xs, cell_ref, lane_ref, force):
    dims, membranes, nodes = pos_ref.shape
    padded = xs.shape[2]
    slab = lax.axis_index("slab")
    cross = lax.axis_index("cross")
    planes, half = plane_count + 2, (columns + 6) // 2

    cell_ref[...] = jnp.full(cell_ref.shape, -1, I32)
    lane_ref[...] = jnp.full(lane_ref.shape, -1, I32)
    plane = pos_ref[0] - (slab * plane_count - 1)
    column = pos_ref[1] - (cross * columns - 3)
    row = pos_ref[2]
    inside = (column >= 0) & (column < 2 * half)
    upper = column >= half
    cell = jnp.where(upper, column - half, column) * planes + plane
    cell_ref[:, :nodes] = jnp.where(inside, cell, -1)
    lane_ref[:, :nodes] = row + jnp.where(upper, rows, 0)

    xs[...] = jnp.zeros_like(xs)
    for k in range(3):
        xs[k, :, :nodes] = (pos_ref[k] - pos_ref[k, :, 0:1]).astype(F32)

    coords = xs[...].reshape(dims * membranes, padded)
    sums = jnp.dot(coords.astype(BF16), inc[...], preferred_element_type=F32)
    tension = ten_ref[...]
    terms = jnp.concatenate(
        [sums[k * membranes : (k + 1) * membranes] * tension for k in range(3)] + [tension], axis=0
    )
    stacked = jnp.concatenate(split(terms, 2), axis=0).astype(BF16)
    gathered = lax.dot_general(stacked, inc[...], NT, preferred_element_type=F32)
    count = terms.shape[0]
    total = gathered[:count] + gathered[count:]
    weight = total[3 * membranes :]
    for k in range(3):
        force[k] = total[k * membranes : (k + 1) * membranes] - 3.0 * xs[k] * weight


def spread_stage(plane_count, columns, cell_ref, lane_ref, force, acc, along, across, out_ref):
    _, membranes, padded = force.shape
    rows = out_ref.shape[2]
    planes, half = plane_count + 2, (columns + 6) // 2
    extent = plane_count + 2 * HALO
    cells = acc.shape[0] // 6
    acc[...] = jnp.zeros_like(acc)
    unroll = 4 if membranes % 4 == 0 else 1
    zero, one = jnp.zeros((), BF16), jnp.ones((), BF16)

    @pl.loop(0, membranes // unroll)
    def _(i):
        running = None
        for inner in range(unroll):
            m = pl.ds(i * unroll + inner, 1)
            cell = cell_ref[m, :].astype(I16)
            lane = lane_ref[m, :].astype(I16)
            mask = lax.broadcasted_iota(I16, (cells, padded), 0) == cell
            values = [split(force[k, m, :], 2) for k in range(3)]
            left = jnp.concatenate(
                [
                    jnp.where(mask, values[k][part].astype(BF16), zero)
                    for part in range(2)
                    for k in range(3)
                ],
                axis=0,
            )
            right = jnp.where(lax.broadcasted_iota(I16, (2 * rows, padded), 0) == lane, one, zero)
            product = lax.dot_general(left, right, NT, preferred_element_type=F32)
            running = product if running is None else running + product
        acc[...] += running

    used = half * planes
    inner = (columns + 4) * planes
    step = lax.broadcasted_iota(I32, (extent, rows), 0)
    weights = [
        jnp.where((step >= 2 - shift) & (step < planes + 2 - shift), w, 0.0)
        for shift, w in ((0, 0.25), (1, 0.5), (2, 0.25))
    ]
    for k in range(3):
        value = acc[k * cells : (k + 1) * cells] + acc[(3 + k) * cells : (4 + k) * cells]
        for part in range(2):
            b = value[:, part * rows : (part + 1) * rows]
            b = 0.5 * b + 0.25 * (pltpu.roll(b, 1, 1) + pltpu.roll(b, rows - 1, 1))
            along[k, part * used : part * used + cells] = b
        across[k, 0:8] = jnp.zeros((8, rows), F32)
        across[k, 8 + inner : 16 + inner] = jnp.zeros((8, rows), F32)
        across[k, 8 : 8 + inner] = 0.5 * along[k, planes : planes + inner] + 0.25 * (
            along[k, 0:inner] + along[k, 2 * planes : 2 * planes + inner]
        )
        for c in range(columns + 4):
            start = 8 + c * planes
            out_ref[k, (c + 1) * extent : (c + 2) * extent] = (
                weights[0] * across[k, start - 2 : start - 2 + extent]
                + weights[1] * across[k, start - 1 : start - 1 + extent]
                + weights[2] * across[k, start : start + extent]
            )


def equilibrium_pairs(density, velocity):
    squared = velocity[0] * velocity[0] + velocity[1] * velocity[1] + velocity[2] * velocity[2]
    base = 1.0 - 1.5 * squared
    result = [None] * 19
    result[0] = LATTICE_WEIGHTS[0] * density * base
    scaled = {w: w * density for w in (1.0 / 18.0, 1.0 / 36.0)}
    for q in range(1, 19, 2):
        projected = None
        for c, v in zip(LATTICE_VECTORS[q], velocity):
            if c == 0:
                continue
            if projected is None:
                projected = v if c == 1 else -v
            else:
                projected = projected + v if c == 1 else projected - v
        even = base + 4.5 * projected * projected
        odd = 3.0 * projected
        weight = scaled[LATTICE_WEIGHTS[q]]
        result[q] = weight * (even + odd)
        result[q + 1] = weight * (even - odd)
    return result


def moments_of(fields):
    density = functools.reduce(lambda a, b: a + b, fields)
    momentum = []
    for k in range(3):
        plus = [fields[q] for q in range(19) if LATTICE_VECTORS[q][k] == 1]
        minus = [fields[q] for q in range(19) if LATTICE_VECTORS[q][k] == -1]
        momentum.append(functools.reduce(lambda a, b: a + b, [a - b for a, b in zip(plus, minus)]))
    return density, momentum


def collide(fields, rate, pushed):
    sums = [fields[q] + fields[q + 1] for q in range(1, 19, 2)]
    gaps = [fields[q] - fields[q + 1] for q in range(1, 19, 2)]
    density = functools.reduce(lambda a, b: a + b, sums) + fields[0]
    scale = 3.0 / density
    tripled = []
    for k in range(3):
        total = pushed[k]
        for pair in range(9):
            c = LATTICE_VECTORS[2 * pair + 1][k]
            if c:
                total = total + gaps[pair] if c == 1 else total - gaps[pair]
        tripled.append(total * scale)
    squared = tripled[0] * tripled[0] + tripled[1] * tripled[1] + tripled[2] * tripled[2]
    base = 1.0 - (1.0 / 6.0) * squared
    fluid = rate > 0.0
    keep = 1.0 - rate
    strength = rate * density
    scaled = {w: w * strength for w in (1.0 / 18.0, 1.0 / 36.0)}
    result = [None] * 19
    rest = keep * fields[0] + (LATTICE_WEIGHTS[0] * strength) * base
    result[0] = jnp.where(fluid, rest, fields[0])
    for q in range(1, 19, 2):
        projected = None
        for c, v in zip(LATTICE_VECTORS[q], tripled):
            if c == 0:
                continue
            if projected is None:
                projected = v if c == 1 else -v
            else:
                projected = projected + v if c == 1 else projected - v
        weight = scaled[LATTICE_WEIGHTS[q]]
        even = weight * (base + 0.5 * projected * projected)
        odd = weight * projected
        result[q] = jnp.where(fluid, keep * fields[q] + (even + odd), fields[q + 1])
        result[q + 1] = jnp.where(fluid, keep * fields[q + 1] + (even - odd), fields[q])
    return result


def lattice_kernel(
    slabs, crosses,
    tri_hbm, pop_hbm, relax_hbm, fluid_hbm, pos_hbm, ten_hbm, coarse_hbm, face_hbm,
    next_ref,
    tri_ref, pop_ref, relax_ref, fluid_ref, pos_ref, ten_ref, coarse_ref, face_ref,
    xs, inc, nodal, cell_ref, lane_ref, acc, along, across,
    raw, own_force, far_force, pushed, placed_ref, rim, post_one, post_two, post_three,
    coarse_all, parts,
    zsend, zrecv, xsend, xrecv, csend, crecv,
    load_sems, coarse_sems, raw_sems, force_sems, placed_sems, halo_sems,
):
    _, plane_count, columns, rows = pop_ref.shape
    extent, wide = plane_count + 2 * HALO, columns + 2 * HALO
    slab = lax.axis_index("slab")
    cross = lax.axis_index("cross")

    def beside(direction, sign):
        dz, dx = direction[0] * sign, direction[1] * sign
        conditions = []
        if dz == 1:
            conditions.append(slab < slabs - 1)
        if dz == -1:
            conditions.append(slab > 0)
        if dx == 1:
            conditions.append(cross < crosses - 1)
        if dx == -1:
            conditions.append(cross > 0)
        return functools.reduce(jnp.logical_and, conditions)

    def target(direction):
        return {"slab": slab + direction[0], "cross": cross + direction[1]}

    def cubed(ref):
        return ref.reshape(ref.shape[0], wide + 2, extent, rows)

    def spans(step, size, depth):
        if step == 1:
            return HALO + size - depth, HALO - depth, depth
        if step == -1:
            return HALO, HALO + size, depth
        return HALO, HALO, size

    def block_copy(ref, sems, index, depth):
        dz, dx = DIRECTIONS[index]
        z_from, z_to, z_size = spans(dz, plane_count, depth)
        x_from, x_to, x_size = spans(dx, columns, depth)
        whole = cubed(ref)
        return pltpu.make_async_remote_copy(
            src_ref=whole.at[:, pl.ds(1 + x_from, x_size), pl.ds(z_from, z_size)],
            dst_ref=whole.at[:, pl.ds(1 + x_to, x_size), pl.ds(z_to, z_size)],
            send_sem=sems.at[0, index],
            recv_sem=sems.at[1, index],
            device_id=target(DIRECTIONS[index]),
            device_id_type=MESH,
        )

    def column_rows(c):
        return pl.ds((c + 1) * extent, extent)

    def plane_rows(p, dz=0, dx=0):
        return pl.ds((HALO + 1 - dx) * extent + HALO + p - dz, columns, stride=extent)

    loads = [
        pltpu.make_async_copy(source, sink, load_sems.at[i])
        for i, (source, sink) in enumerate(
            (
                (tri_hbm, tri_ref),
                (pop_hbm, pop_ref),
                (relax_hbm, relax_ref),
                (fluid_hbm, fluid_ref),
                (pos_hbm, pos_ref),
                (ten_hbm, ten_ref),
                (coarse_hbm, coarse_ref),
                (face_hbm, face_ref),
            )
        )
    ]
    for load in loads:
        load.start()

    barrier = pltpu.get_barrier_semaphore()

    @pl.loop(1, slabs)
    def _(d):
        peer = lax.rem(slab + d, slabs)
        pl.semaphore_signal(
            barrier, inc=1, device_id={"slab": peer, "cross": cross}, device_id_type=MESH
        )

    expected = slabs - 1
    for direction in DIRECTIONS:
        if direction[1] == 0:
            continue
        there = beside(direction, 1)
        expected = expected + jnp.where(there, 1, 0)

        @pl.when(there)
        def _():
            pl.semaphore_signal(
                barrier, inc=1, device_id=target(direction), device_id_type=MESH
            )

    def clear(side):
        dz, dx = DIRECTIONS[side]
        for c in range(-1, wide + 1):
            if dx == 1 and c >= HALO or dx == -1 and c < HALO + columns:
                continue
            start = (c + 1) * extent
            if dz == 1:
                start, size = start, HALO
            elif dz == -1:
                start, size = start + HALO + plane_count, HALO
            else:
                size = extent
            for q in range(20):
                raw[q, pl.ds(start, size), :] = jnp.zeros((size, rows), F32)
            for q in range(5):
                placed_ref[q, pl.ds(start, size), :] = jnp.full((size, rows), 1.0 if q == 4 else 0.0, F32)
        if dx == 0:
            zrecv[side] = jnp.zeros(zrecv.shape[1:], F32)
            near = 0 if dz == 1 else extent // 2
            for c in range(wide):
                for k in range(3):
                    far_force[k, pl.ds((c + 1) * extent + near, extent // 2), :] = jnp.zeros(
                        (extent // 2, rows), F32
                    )
        else:
            xrecv[side - 2] = jnp.zeros(xrecv.shape[1:], F32)

    for side in range(4):

        @pl.when(jnp.logical_not(beside(DIRECTIONS[side], -1)))
        def _():
            clear(side)

    for index in range(4):

        @pl.when(jnp.logical_not(beside(DIRECTIONS[4 + index], -1)))
        def _():
            crecv[index] = jnp.zeros(crecv.shape[1:], F32)

    loads[0].wait()
    incidence_stage(tri_ref, inc, pos_ref.shape[2])
    for load in loads[1:4]:
        load.wait()
    for p in range(plane_count):
        for q in range(19):
            raw[q, plane_rows(p), :] = pop_ref[q, p]
        raw[19, plane_rows(p), :] = jnp.where(fluid_ref[p] == 1, relax_ref[p], 0.0)
    loads[6].wait()
    pl.semaphore_wait(barrier, expected)

    for index in (4, 5, 6, 7, 0, 1, 2, 3):

        @pl.when(beside(DIRECTIONS[index], 1))
        def _():
            block_copy(raw, raw_sems, index, HALO).start()

    coarse_all[slab] = coarse_ref[...]

    def coarse_copy(d):
        return pltpu.make_async_remote_copy(
            src_ref=coarse_ref,
            dst_ref=coarse_all.at[slab],
            send_sem=coarse_sems.at[0, d],
            recv_sem=coarse_sems.at[1, d],
            device_id={"slab": lax.rem(slab + d, slabs), "cross": cross},
            device_id_type=MESH,
        )

    @pl.loop(1, slabs)
    def _(d):
        coarse_copy(d).start()

    for load in loads[4:6]:
        load.wait()
    nodal_stage(
        plane_count, columns, rows, pos_ref, ten_ref, inc, xs, cell_ref, lane_ref, nodal
    )
    spread_stage(plane_count, columns, cell_ref, lane_ref, nodal, acc, along, across, own_force)

    def force_copy(index):
        part = extent // 2
        start = part if index == 0 else 0
        return pltpu.make_async_remote_copy(
            src_ref=cubed(own_force).at[:, pl.ds(1, wide), pl.ds(start, part)],
            dst_ref=cubed(far_force).at[:, pl.ds(1, wide), pl.ds(part - start, part)],
            send_sem=force_sems.at[0, index],
            recv_sem=force_sems.at[1, index],
            device_id=target(DIRECTIONS[index]),
            device_id_type=MESH,
        )

    for index in range(2):

        @pl.when(beside(DIRECTIONS[index], 1))
        def _():
            force_copy(index).start()

    loads[7].wait()
    cell = face_ref[pl.ds(0, 1), :]
    slots = cell.shape[1]
    used = cell >= 0
    place = cell // rows
    place = jnp.where(used, place % columns * plane_count + place // columns, -1)
    lane = jnp.where(used, cell % rows, -1)
    first = face_ref[pl.ds(1, 1), :]
    second = face_ref[pl.ds(2, 1), :]
    width = coarse_ref.shape[1]

    @pl.loop(1, slabs)
    def _(d):
        pltpu.make_async_remote_copy(
            src_ref=coarse_ref,
            dst_ref=coarse_all.at[lax.rem(slab + slabs - d, slabs)],
            send_sem=coarse_sems.at[0, d],
            recv_sem=coarse_sems.at[1, d],
            device_id={"slab": lax.rem(slab + d, slabs), "cross": cross},
            device_id_type=MESH,
        ).wait_recv()

    parts[...] = jnp.zeros_like(parts)
    zero = jnp.zeros((), BF16)

    def local(index, j):
        at = index - j * width
        return jnp.where((at >= 0) & (at < width), at, -1).astype(I16)

    def blend(j, running):
        for i, piece in enumerate(split(coarse_all[j], 2)):
            parts[pl.ds(8 * i, 4), :] = piece
        ids = lax.broadcasted_iota(I16, (width, slots), 0)
        table = jnp.where(ids == local(first, j), jnp.full((), 0.75, BF16), zero) + jnp.where(
            ids == local(second, j), jnp.full((), 0.25, BF16), zero
        )
        return running + jnp.dot(parts[...].astype(BF16), table, preferred_element_type=F32)

    mixed = lax.fori_loop(0, slabs, blend, jnp.zeros((16, slots), F32))
    blended = mixed[0:4] + mixed[8:12]

    cells = plane_count * columns
    mask = lax.broadcasted_iota(I32, (cells, slots), 0) == place
    pieces = split(blended, 2)
    left = [jnp.where(mask, piece[m : m + 1], 0.0) for m in range(4) for piece in pieces]
    left.append(jnp.where(mask, 1.0, 0.0))
    right = jnp.where(lax.broadcasted_iota(I32, (rows, slots), 0) == lane, 1.0, 0.0)
    placed = lax.dot_general(
        jnp.concatenate(left, axis=0).astype(BF16), right.astype(BF16), NT, preferred_element_type=F32
    )
    for m in range(5):
        value = placed[2 * m * cells : (2 * m + 1) * cells]
        if m < 4:
            value = value + placed[(2 * m + 1) * cells : (2 * m + 2) * cells]
        for c in range(columns):
            placed_ref[m, pl.ds((HALO + 1 + c) * extent + HALO, plane_count), :] = value[
                c * plane_count : (c + 1) * plane_count
            ]

    for index in (4, 5, 6, 7, 0, 1, 2, 3):

        @pl.when(beside(DIRECTIONS[index], 1))
        def _():
            block_copy(placed_ref, placed_sems, index, 1).start()

    for index in range(8):

        @pl.when(beside(DIRECTIONS[index], -1))
        def _():
            block_copy(placed_ref, placed_sems, index, 1).wait_recv()

    for c in range(1, wide - 1):
        at = column_rows(c)
        density = placed_ref[0, at, :]
        velocity = [placed_ref[k, at, :] for k in range(1, 4)]
        for q, value in enumerate(equilibrium_pairs(density, velocity)):
            rim[q, at, :] = value

    for index in range(2):

        @pl.when(beside(DIRECTIONS[index], -1))
        def _():
            force_copy(index).wait_recv()

    for index in range(8):

        @pl.when(beside(DIRECTIONS[index], -1))
        def _():
            block_copy(raw, raw_sems, index, HALO).wait_recv()

    def pulled(source, at, starts):
        fixed = placed_ref[4, at, :] > 0.5
        fields = []
        for q, (cz, cx, cy) in enumerate(LATTICE_VECTORS):
            value = source[q, starts(cz, cx), :]
            if cy != 0:
                value = pltpu.roll(value, cy % rows, 1)
            fields.append(jnp.where(fixed, rim[q, at, :], value))
        return fields

    def pulled_column(source, c):
        return pulled(
            source,
            column_rows(c),
            lambda cz, cx: pl.ds((c + 1 - cx) * extent - cz, extent),
        )

    def pulled_plane(source, p):
        return pulled(source, plane_rows(p), lambda cz, cx: plane_rows(p, cz, cx))

    for c in range(wide):
        at = column_rows(c)
        rate = raw[19, at, :]
        fluid = rate > 0.0
        inverse = 1.0 / rate
        push = []
        for k in range(3):
            value = jnp.where(fluid, (own_force[k, at, :] + far_force[k, at, :]) * inverse, 0.0)
            pushed[k, at, :] = value
            push.append(value)
        for q, value in enumerate(collide([raw[q, at, :] for q in range(19)], rate, push)):
            post_one[q, at, :] = value

    def collide_columns(source, sink):
        for c in range(1, wide - 1):
            at = column_rows(c)
            fields = pulled_column(source, c)
            push = [pushed[k, at, :] for k in range(3)]
            for q, value in enumerate(collide(fields, raw[19, at, :], push)):
                sink[q, at, :] = value

    collide_columns(post_one, post_two)

    for p in range(plane_count):
        at = plane_rows(p)
        fields = pulled_plane(post_two, p)
        push = [pushed[k, at, :] for k in range(3)]
        for q, value in enumerate(collide(fields, raw[19, at, :], push)):
            post_three[q, at, :] = value
            for side in range(2):
                depth = plane_count - p if side == 0 else p + 1
                if (q, depth) in SLAB_MOVES[side]:
                    zsend[side, SLAB_MOVES[side].index((q, depth))] = value

    def inner_row(step, depth, size):
        return HALO + (size - depth if step == 1 else depth - 1)

    def outer_row(step, depth, size):
        return HALO + (-depth if step == 1 else size - 1 + depth)

    for side in range(4):
        for e, (q, dz, dx) in enumerate(CORNER_MOVES[side]):
            sz, sx = DIRECTIONS[4 + side]
            row = (inner_row(sx, dx, columns) + 1) * extent + inner_row(sz, dz, plane_count)
            csend[side, pl.ds(e, 1), :] = post_three[q, pl.ds(row, 1), :]
    for side in range(2):
        for e, (q, depth) in enumerate(CROSS_MOVES[side]):
            row = (inner_row(DIRECTIONS[2 + side][1], depth, columns) + 1) * extent + HALO
            xsend[side, pl.ds(e * plane_count, plane_count), :] = post_three[
                q, pl.ds(row, plane_count), :
            ]

    def halo_copy(index):
        if index < 2:
            source, sink = zsend.at[index], zrecv.at[index]
        elif index < 4:
            source, sink = xsend.at[index - 2], xrecv.at[index - 2]
        else:
            source, sink = csend.at[index - 4], crecv.at[index - 4]
        return pltpu.make_async_remote_copy(
            src_ref=source,
            dst_ref=sink,
            send_sem=halo_sems.at[0, index],
            recv_sem=halo_sems.at[1, index],
            device_id=target(DIRECTIONS[index]),
            device_id_type=MESH,
        )

    for index in (4, 5, 6, 7, 0, 1, 2, 3):

        @pl.when(beside(DIRECTIONS[index], 1))
        def _():
            halo_copy(index).start()

    for index in range(8):

        @pl.when(beside(DIRECTIONS[index], -1))
        def _():
            halo_copy(index).wait_recv()

    for side in range(2):
        for e, (q, depth) in enumerate(SLAB_MOVES[side]):
            row = outer_row(DIRECTIONS[side][0], depth, plane_count)
            post_three[q, plane_rows(row - HALO), :] = zrecv[side, e]
        for e, (q, depth) in enumerate(CROSS_MOVES[side]):
            row = (outer_row(DIRECTIONS[2 + side][1], depth, columns) + 1) * extent + HALO
            post_three[q, pl.ds(row, plane_count), :] = xrecv[
                side, pl.ds(e * plane_count, plane_count), :
            ]
    for side in range(4):
        for e, (q, dz, dx) in enumerate(CORNER_MOVES[side]):
            sz, sx = DIRECTIONS[4 + side]
            row = (outer_row(sx, dx, columns) + 1) * extent + outer_row(sz, dz, plane_count)
            post_three[q, pl.ds(row, 1), :] = crecv[side, pl.ds(e, 1), :]

    collide_columns(post_three, post_one)

    for p in range(plane_count):
        for q, value in enumerate(pulled_plane(post_one, p)):
            next_ref[q, p] = value

    @pl.loop(1, slabs)
    def _(d):
        coarse_copy(d).wait_send()

    for index in range(8):

        @pl.when(beside(DIRECTIONS[index], 1))
        def _():
            block_copy(raw, raw_sems, index, HALO).wait_send()
            block_copy(placed_ref, placed_sems, index, 1).wait_send()
            halo_copy(index).wait_send()
            if index < 2:
                force_copy(index).wait_send()


def flow_kernel(fields_ref, next_ref, flow_ref, flow, sems):
    whole = pltpu.make_async_copy(fields_ref, next_ref, sems.at[0])
    whole.start()
    for p in range(fields_ref.shape[1]):
        fields = [fields_ref[q, p] for q in range(19)]
        density, momentum = moments_of(fields)
        inverse = ROOT_THREE / density
        for k in range(3):
            flow[k, p] = momentum[k] * inverse
    part = pltpu.make_async_copy(flow, flow_ref, sems.at[1])
    part.start()
    whole.wait()
    part.wait()


def on_device(
    slabs, crosses,
    populations, fluid_mask, relaxation, positions, triangles, tension, coarse_moments, interface,
):
    _, plane_count, columns, rows = populations.shape
    _, membranes, nodes = positions.shape
    padded = round_up(nodes, 128)
    corners = triangles.shape[1]
    half, planes = (columns + 6) // 2, plane_count + 2
    cells = round_up(planes * half, 16)
    flat = (columns + 2 * HALO + 2) * (plane_count + 2 * HALO)
    vmem = pl.BlockSpec(memory_space=pltpu.VMEM)
    block = (19, plane_count, columns, rows)
    operands = (
        triangles, populations, relaxation, fluid_mask, positions, tension, coarse_moments, interface,
    )
    fields = pl.pallas_call(
        functools.partial(lattice_kernel, slabs, crosses),
        name="lattice_steps",
        out_shape=pltpu.VMEM(block, F32),
        in_specs=[pl.BlockSpec(memory_space=pl.ANY)] * 8,
        out_specs=vmem,
        scratch_shapes=[pltpu.VMEM(operand.shape, operand.dtype) for operand in operands]
        + [
            pltpu.VMEM((3, membranes, padded), F32),
            pltpu.VMEM((padded, corners), BF16),
            pltpu.VMEM((3, membranes, padded), F32),
            pltpu.VMEM((membranes, padded), I32),
            pltpu.VMEM((membranes, padded), I32),
            pltpu.VMEM((6 * cells, 2 * rows), F32),
            pltpu.VMEM((3, half * planes + cells, rows), F32),
            pltpu.VMEM((3, (columns + 4) * planes + 16, rows), F32),
            pltpu.VMEM((20, flat, rows), F32),
            pltpu.VMEM((3, flat, rows), F32),
            pltpu.VMEM((3, flat, rows), F32),
            pltpu.VMEM((3, flat, rows), F32),
            pltpu.VMEM((5, flat, rows), F32),
            pltpu.VMEM((19, flat, rows), F32),
            pltpu.VMEM((19, flat, rows), F32),
            pltpu.VMEM((19, flat, rows), F32),
            pltpu.VMEM((19, flat, rows), F32),
            pltpu.VMEM((slabs,) + coarse_moments.shape, F32),
            pltpu.VMEM((16, coarse_moments.shape[1]), F32),
            pltpu.VMEM((2, 19, columns, rows), F32),
            pltpu.VMEM((2, 19, columns, rows), F32),
            pltpu.VMEM((2, round_up(19 * plane_count, 8), rows), F32),
            pltpu.VMEM((2, round_up(19 * plane_count, 8), rows), F32),
            pltpu.VMEM((4, 24, rows), F32),
            pltpu.VMEM((4, 24, rows), F32),
            pltpu.SemaphoreType.DMA((8,)),
            pltpu.SemaphoreType.DMA((2, slabs)),
            pltpu.SemaphoreType.DMA((2, 8)),
            pltpu.SemaphoreType.DMA((2, 2)),
            pltpu.SemaphoreType.DMA((2, 8)),
            pltpu.SemaphoreType.DMA((2, 8)),
        ],
        compiler_params=pltpu.CompilerParams(collective_id=0, has_side_effects=True),
    )(*operands)
    return pl.pallas_call(
        flow_kernel,
        name="flow",
        out_shape=(
            jax.ShapeDtypeStruct(block, F32),
            jax.ShapeDtypeStruct((3,) + block[1:], F32),
        ),
        in_specs=[vmem],
        out_specs=(pl.BlockSpec(memory_space=pl.ANY),) * 2,
        scratch_shapes=[pltpu.VMEM((3,) + block[1:], F32), pltpu.SemaphoreType.DMA((2,))],
    )(pltpu.with_memory_space_constraint(fields, pltpu.VMEM))


def solution(mesh):
    in_specs = (
        P(None, "slab", "cross", None),
        P("slab", "cross", None),
        P("slab", "cross", None),
        P(None, "slab", None),
        P(),
        P("slab", None),
        P(None, "slab"),
        P(None, ("slab", "cross")),
    )
    out_specs = (P(None, "slab", "cross", None), P(None, "slab", "cross", None))
    return jax.shard_map(
        functools.partial(on_device, mesh.shape["slab"], mesh.shape["cross"]),
        mesh=mesh, in_specs=in_specs, out_specs=out_specs, check_vma=False,
    )
```

time: 26.2 us -> 25.2 us (0.962)
  the two profiles are of different devices: /device:TPU:11 before, /device:TPU:0 now
where the time goes in v2:
time: 25.2 us; the launch traced here: 25.1 us
  Pallas kernels  24.5 us (97%)
  between operations  0.64 us (3%)
    pallas_call x1, Pallas kernels, on_device(): pl.pallas_call(functools.partial(lattice_kernel, slabs, crosses), name='l...  23.7 us
    pallas_call x1, Pallas kernels, on_device(): pl.pallas_call(flow_kernel, name='flow', out_shape=(jax.ShapeDtypeStruct(...  0.74 us

profile of v2, /device:TPU:0, one launch (start us, length us, event | category | flops | bytes accessed | tf_op | source)
XLA Modules:
  0.0 25.1 jit_solution(7061517856090202044)
XLA Ops:
  0.6 23.7 %lattice_steps.1.fields_ref = f32[19,4,8,128]{3,2,1,0:T(8,128)S(1)} custom-call(s32[3,1280]{1,0:T(4,128)} %tri_hbm.1, f32[19,4,8,128]{3,2,1,0:T(8,128)} %pop_hbm.1, f32[4,8,128]{2,1,0:T(8,128)} %relax_hbm.1, s32[4,8,128]{2,1,0:T(8,128)} %fluid_hbm.1, s32[3,16,642]{2,1,0:T(8,128)} %pos_hbm.1, f32[16,1280]{1,0:T(8,128)} %ten_hbm.1, f32[4,512]{1,0:T(4,128)} %coarse_hbm.1, ...), custom_call_target="tpu_custom_call" | custom-call | tf_op jit(solution)/shard_map/lattice_steps/pallas_call | solution.py:733
  24.4 0.7 %flow.1 = (f32[19,4,8,128]{3,2,1,0:T(8,128)}, f32[3,4,8,128]{3,2,1,0:T(8,128)}) custom-call(f32[19,4,8,128]{3,2,1,0:T(8,128)S(1)} %lattice_steps.1.fields_ref), custom_call_target="tpu_custom_call" | custom-call | tf_op jit(solution)/shard_map/flow/pallas_call | solution.py:775

commit v3 on v2

--- a/solution.py
+++ b/solution.py
@@ -281,9 +281,9 @@
     tri_ref, pop_ref, relax_ref, fluid_ref, pos_ref, ten_ref, coarse_ref, face_ref,
     xs, inc, nodal, cell_ref, lane_ref, acc, along, across,
     raw, own_force, far_force, pushed, placed_ref, rim, post_one, post_two, post_three,
-    coarse_all, parts,
+    coarse_all, table, faces,
     zsend, zrecv, xsend, xrecv, csend, crecv,
-    load_sems, coarse_sems, raw_sems, force_sems, placed_sems, halo_sems,
+    load_sems, coarse_sems, raw_sems, force_sems, face_sems, halo_sems,
 ):
     _, plane_count, columns, rows = pop_ref.shape
     extent, wide = plane_count + 2 * HALO, columns + 2 * HALO
@@ -390,8 +390,6 @@
                 size = extent
             for q in range(20):
                 raw[q, pl.ds(start, size), :] = jnp.zeros((size, rows), F32)
-            for q in range(5):
-                placed_ref[q, pl.ds(start, size), :] = jnp.full((size, rows), 1.0 if q == 4 else 0.0, F32)
         if dx == 0:
             zrecv[side] = jnp.zeros(zrecv.shape[1:], F32)
             near = 0 if dz == 1 else extent // 2
@@ -409,28 +407,18 @@
         def _():
             clear(side)
 
-    for index in range(4):
-
-        @pl.when(jnp.logical_not(beside(DIRECTIONS[4 + index], -1)))
-        def _():
-            crecv[index] = jnp.zeros(crecv.shape[1:], F32)
+    for index in range(8):
+
+        @pl.when(jnp.logical_not(beside(DIRECTIONS[index], -1)))
+        def _():
+            faces[index] = jnp.full(faces.shape[1:], -1, I32)
+            if index >= 4:
+                crecv[index - 4] = jnp.zeros(crecv.shape[1:], F32)
 
     loads[0].wait()
     incidence_stage(tri_ref, inc, pos_ref.shape[2])
-    for load in loads[1:4]:
-        load.wait()
-    for p in range(plane_count):
-        for q in range(19):
-            raw[q, plane_rows(p), :] = pop_ref[q, p]
-        raw[19, plane_rows(p), :] = jnp.where(fluid_ref[p] == 1, relax_ref[p], 0.0)
     loads[6].wait()
     pl.semaphore_wait(barrier, expected)
-
-    for index in (4, 5, 6, 7, 0, 1, 2, 3):
-
-        @pl.when(beside(DIRECTIONS[index], 1))
-        def _():
-            block_copy(raw, raw_sems, index, HALO).start()
 
     coarse_all[slab] = coarse_ref[...]
 
@@ -447,6 +435,36 @@
     @pl.loop(1, slabs)
     def _(d):
         coarse_copy(d).start()
+
+    loads[7].wait()
+
+    def face_copy(index):
+        return pltpu.make_async_remote_copy(
+            src_ref=face_ref,
+            dst_ref=faces.at[index],
+            send_sem=face_sems.at[0, index],
+            recv_sem=face_sems.at[1, index],
+            device_id=target(DIRECTIONS[index]),
+            device_id_type=MESH,
+        )
+
+    for index in (4, 5, 6, 7, 0, 1, 2, 3):
+
+        @pl.when(beside(DIRECTIONS[index], 1))
+        def _():
+            face_copy(index).start()
+
+    for load in loads[1:4]:
+        load.wait()
+    for p in range(plane_count):
+        for q in range(19):
+            raw[q, plane_rows(p), :] = pop_ref[q, p]
+        raw[19, plane_rows(p), :] = jnp.where(fluid_ref[p] == 1, relax_ref[p], 0.0)
+    for index in (4, 5, 6, 7, 0, 1, 2, 3):
+
+        @pl.when(beside(DIRECTIONS[index], 1))
+        def _():
+            block_copy(raw, raw_sems, index, HALO).start()
 
     for load in loads[4:6]:
         load.wait()
@@ -473,17 +491,6 @@
         def _():
             force_copy(index).start()
 
-    loads[7].wait()
-    cell = face_ref[pl.ds(0, 1), :]
-    slots = cell.shape[1]
-    used = cell >= 0
-    place = cell // rows
-    place = jnp.where(used, place % columns * plane_count + place // columns, -1)
-    lane = jnp.where(used, cell % rows, -1)
-    first = face_ref[pl.ds(1, 1), :]
-    second = face_ref[pl.ds(2, 1), :]
-    width = coarse_ref.shape[1]
-
     @pl.loop(1, slabs)
     def _(d):
         pltpu.make_async_remote_copy(
@@ -495,54 +502,127 @@
             device_id_type=MESH,
         ).wait_recv()
 
-    parts[...] = jnp.zeros_like(parts)
-    zero = jnp.zeros((), BF16)
-
-    def local(index, j):
-        at = index - j * width
-        return jnp.where((at >= 0) & (at < width), at, -1).astype(I16)
-
-    def blend(j, running):
-        for i, piece in enumerate(split(coarse_all[j], 2)):
-            parts[pl.ds(8 * i, 4), :] = piece
-        ids = lax.broadcasted_iota(I16, (width, slots), 0)
-        table = jnp.where(ids == local(first, j), jnp.full((), 0.75, BF16), zero) + jnp.where(
-            ids == local(second, j), jnp.full((), 0.25, BF16), zero
-        )
-        return running + jnp.dot(parts[...].astype(BF16), table, preferred_element_type=F32)
-
-    mixed = lax.fori_loop(0, slabs, blend, jnp.zeros((16, slots), F32))
-    blended = mixed[0:4] + mixed[8:12]
-
-    cells = plane_count * columns
-    mask = lax.broadcasted_iota(I32, (cells, slots), 0) == place
-    pieces = split(blended, 2)
-    left = [jnp.where(mask, piece[m : m + 1], 0.0) for m in range(4) for piece in pieces]
-    left.append(jnp.where(mask, 1.0, 0.0))
-    right = jnp.where(lax.broadcasted_iota(I32, (rows, slots), 0) == lane, 1.0, 0.0)
-    placed = lax.dot_general(
-        jnp.concatenate(left, axis=0).astype(BF16), right.astype(BF16), NT, preferred_element_type=F32
+    for index in range(8):
+
+        @pl.when(beside(DIRECTIONS[index], -1))
+        def _():
+            face_copy(index).wait_recv()
+
+    slots = face_ref.shape[1]
+    lanes = table.shape[1]
+    chunks = coarse_ref.shape[1] // lanes
+    together = table.shape[0] // (4 * chunks)
+    groups = [[face_ref[pl.ds(k, 1), :] for k in range(3)]] + [
+        [faces[index, pl.ds(k, 1), :] for k in range(3)] for index in range(8)
+    ]
+    wanted = [jnp.concatenate(group[1:], axis=1) for group in groups]
+    one, zero = jnp.ones((), BF16), jnp.zeros((), BF16)
+    picks = [
+        jnp.where(
+            lax.broadcasted_iota(I16, (lanes, 2 * slots), 0) == (index & (lanes - 1)).astype(I16),
+            one, zero,
+        )
+        for index in wanted
+    ]
+    quarter = lax.shift_right_logical(
+        lax.broadcasted_iota(I32, (table.shape[0], 2 * slots), 0), 2
     )
-    for m in range(5):
-        value = placed[2 * m * cells : (2 * m + 1) * cells]
-        if m < 4:
-            value = value + placed[(2 * m + 1) * cells : (2 * m + 2) * cells]
+
+    def gather(base, found):
+        for j in range(together):
+            for chunk in range(chunks):
+                table[pl.ds((j * chunks + chunk) * 4, 4), :] = coarse_all[
+                    base * together + j, :, chunk * lanes : (chunk + 1) * lanes
+                ]
+        stacked = jnp.concatenate(split(table[...], 2), axis=0).astype(BF16)
+        result = []
+        for index, pick, total in zip(wanted, picks, found):
+            both = jnp.dot(stacked, pick, preferred_element_type=F32)
+            both = both[: table.shape[0]] + both[table.shape[0] :]
+            high = lax.shift_right_logical(index, lanes.bit_length() - 1)
+            both = jnp.where(quarter == high - base * (together * chunks), both, 0.0)
+            for start in range(0, table.shape[0], 8):
+                total = total + both[start : start + 8]
+            result.append(total)
+        return tuple(result)
+
+    found = tuple(jnp.zeros((8, 2 * slots), F32) for _ in groups)
+    if coarse_all.shape[0] == together:
+        found = gather(0, found)
+    else:
+        found = lax.fori_loop(0, coarse_all.shape[0] // together, gather, found)
+    blended = []
+    for total in found:
+        total = total[0:4] + total[4:8]
+        blended.append(0.75 * total[:, :slots] + 0.25 * total[:, slots:])
+
+    def spots(group):
+        cell = group[0]
+        used = cell >= 0
+        line = cell // rows
+        return used, line // columns, line % columns, jnp.where(used, cell % rows, -1)
+
+    def put(size, goals, lane_rows, moments):
+        mask = [lax.broadcasted_iota(I32, (size, slots), 0) == goal for goal in goals]
+        pieces = [split(value, 2) for value in moments]
+        left = [
+            jnp.concatenate(
+                [jnp.where(m, piece[part][k : k + 1], 0.0) for m, piece in zip(mask, pieces)], axis=1
+            )
+            for k in range(4)
+            for part in range(2)
+        ]
+        left.append(jnp.concatenate([jnp.where(m, 1.0, 0.0) for m in mask], axis=1))
+        right = jnp.concatenate(
+            [
+                jnp.where(lax.broadcasted_iota(I32, (rows, slots), 0) == lane, 1.0, 0.0)
+                for lane in lane_rows
+            ],
+            axis=1,
+        )
+        out = lax.dot_general(
+            jnp.concatenate(left, axis=0).astype(BF16), right.astype(BF16), NT,
+            preferred_element_type=F32,
+        )
+        return [
+            out[2 * k * size : (2 * k + 1) * size] + out[(2 * k + 1) * size : (2 * k + 2) * size]
+            for k in range(4)
+        ] + [out[8 * size : 9 * size]]
+
+    used, plane, column, lane = spots(groups[0])
+    goal = jnp.where(used, column * plane_count + plane, -1)
+    for k, value in enumerate(put(columns * plane_count, [goal], [lane], blended[:1])):
         for c in range(columns):
-            placed_ref[m, pl.ds((HALO + 1 + c) * extent + HALO, plane_count), :] = value[
+            placed_ref[k, pl.ds((HALO + 1 + c) * extent + HALO, plane_count), :] = value[
                 c * plane_count : (c + 1) * plane_count
             ]
 
-    for index in (4, 5, 6, 7, 0, 1, 2, 3):
-
-        @pl.when(beside(DIRECTIONS[index], 1))
-        def _():
-            block_copy(placed_ref, placed_sems, index, 1).start()
-
-    for index in range(8):
-
-        @pl.when(beside(DIRECTIONS[index], -1))
-        def _():
-            block_copy(placed_ref, placed_sems, index, 1).wait_recv()
+    goals, lane_rows, offsets, offset = [], [], [], 0
+    for index, (dz, dx) in enumerate(DIRECTIONS):
+        used, plane, column, lane = spots(groups[1 + index])
+        if dz:
+            used = used & (plane == (plane_count - 1 if dz == 1 else 0))
+        if dx:
+            used = used & (column == (columns - 1 if dx == 1 else 0))
+        along_edge = column if dx == 0 else plane if dz == 0 else jnp.zeros_like(plane)
+        goals.append(jnp.where(used, along_edge + offset, -1))
+        lane_rows.append(lane)
+        offsets.append(offset)
+        offset += columns if dx == 0 else plane_count if dz == 0 else 1
+    for k, value in enumerate(put(round_up(offset, 16), goals, lane_rows, blended[1:])):
+        for index, (dz, dx) in enumerate(DIRECTIONS):
+            size = columns if dx == 0 else plane_count if dz == 0 else 1
+            part = value[offsets[index] : offsets[index] + size]
+            if k == 4:
+                part = jnp.where(beside(DIRECTIONS[index], -1), part, 1.0)
+            p = -1 if dz == 1 else plane_count
+            c = HALO + (-1 if dx == 1 else columns)
+            if dx == 0:
+                placed_ref[k, plane_rows(p), :] = part
+            elif dz == 0:
+                placed_ref[k, pl.ds((c + 1) * extent + HALO, plane_count), :] = part
+            else:
+                placed_ref[k, pl.ds((c + 1) * extent + HALO + p, 1), :] = part
 
     for c in range(1, wide - 1):
         at = column_rows(c)
@@ -693,7 +773,7 @@
         @pl.when(beside(DIRECTIONS[index], 1))
         def _():
             block_copy(raw, raw_sems, index, HALO).wait_send()
-            block_copy(placed_ref, placed_sems, index, 1).wait_send()
+            face_copy(index).wait_send()
             halo_copy(index).wait_send()
             if index < 2:
                 force_copy(index).wait_send()
@@ -712,6 +792,11 @@
     part.start()
     whole.wait()
     part.wait()
+
+
+def coarse_rows(slabs, coarse_moments):
+    count, width = coarse_moments.shape
+    return math.gcd(slabs, 8) * count * (width // 128)
 
 
 def on_device(
@@ -756,7 +841,8 @@
             pltpu.VMEM((19, flat, rows), F32),
             pltpu.VMEM((19, flat, rows), F32),
             pltpu.VMEM((slabs,) + coarse_moments.shape, F32),
-            pltpu.VMEM((16, coarse_moments.shape[1]), F32),
+            pltpu.VMEM((coarse_rows(slabs, coarse_moments), 128), F32),
+            pltpu.VMEM((8,) + interface.shape, I32),
             pltpu.VMEM((2, 19, columns, rows), F32),
             pltpu.VMEM((2, 19, columns, rows), F32),
             pltpu.VMEM((2, round_up(19 * plane_count, 8), rows), F32),

time: 25.2 us -> 20.3 us (0.81)
  the two profiles are of different devices: /device:TPU:0 before, /device:TPU:11 now
where the time goes in v3:
time: 20.3 us; the launch traced here: 20.1 us
  Pallas kernels  19.5 us (96%)
  between operations  0.64 us (3%)
    pallas_call x1, Pallas kernels, on_device(): pl.pallas_call(functools.partial(lattice_kernel, slabs, crosses), name='l...  18.8 us
    pallas_call x1, Pallas kernels, on_device(): pl.pallas_call(flow_kernel, name='flow', out_shape=(jax.ShapeDtypeStruct(...  0.74 us

profile of v3, /device:TPU:11, one launch (start us, length us, event | category | flops | bytes accessed | tf_op | source)
XLA Modules:
  0.0 20.1 jit_solution(6866772973724999787)
XLA Ops:
  0.6 18.8 %lattice_steps.1.fields_ref = f32[19,4,8,128]{3,2,1,0:T(8,128)S(1)} custom-call(s32[3,1280]{1,0:T(4,128)} %tri_hbm.1, f32[19,4,8,128]{3,2,1,0:T(8,128)} %pop_hbm.1, f32[4,8,128]{2,1,0:T(8,128)} %relax_hbm.1, s32[4,8,128]{2,1,0:T(8,128)} %fluid_hbm.1, s32[3,16,642]{2,1,0:T(8,128)} %pos_hbm.1, f32[16,1280]{1,0:T(8,128)} %ten_hbm.1, f32[4,512]{1,0:T(4,128)} %coarse_hbm.1, ...), custom_call_target="tpu_custom_call" | custom-call | tf_op jit(solution)/shard_map/lattice_steps/pallas_call | solution.py:818
  19.4 0.7 %flow.1 = (f32[19,4,8,128]{3,2,1,0:T(8,128)}, f32[3,4,8,128]{3,2,1,0:T(8,128)}) custom-call(f32[19,4,8,128]{3,2,1,0:T(8,128)S(1)} %lattice_steps.1.fields_ref), custom_call_target="tpu_custom_call" | custom-call | tf_op jit(solution)/shard_map/flow/pallas_call | solution.py:861

commit v4 on v3

--- a/solution.py
+++ b/solution.py
@@ -38,24 +38,59 @@
 NT = (((1,), (1,)), ((), ()))
 F32, BF16, I32, I16 = jnp.float32, jnp.bfloat16, jnp.int32, jnp.int16
 HALO = 2
-SLAB_MOVES = [
-    [(q, depth) for depth in (1, 2) for q in range(19) if LATTICE_VECTORS[q][0] * sign >= depth - 1]
-    for sign in (1, -1)
-]
-CROSS_MOVES = [
-    [(q, depth) for depth in (1, 2) for q in range(19) if LATTICE_VECTORS[q][1] * sign >= depth - 1]
-    for sign in (1, -1)
-]
-CORNER_MOVES = [
-    [
-        (q, dz, dx)
-        for dz in (1, 2)
-        for dx in (1, 2)
-        for q in range(19)
-        if LATTICE_VECTORS[q][0] * sz >= dz - 1 and LATTICE_VECTORS[q][1] * sx >= dx - 1
+
+
+def slab_moves(extra):
+    return [
+        [
+            (q, depth)
+            for depth in (1, 2)
+            for q in [m for m in range(19) if LATTICE_VECTORS[m][0] * sign >= depth - 1] + extra
+        ]
+        for sign in (1, -1)
     ]
-    for sz, sx in DIRECTIONS[4:]
-]
+
+
+def cross_moves(extra):
+    return [
+        [
+            (q, depth)
+            for depth in (1, 2)
+            for q in [m for m in range(19) if LATTICE_VECTORS[m][1] * sign >= depth - 1] + extra
+        ]
+        for sign in (1, -1)
+    ]
+
+
+def corner_moves(extra):
+    return [
+        [
+            (q, dz, dx)
+            for dz in (1, 2)
+            for dx in (1, 2)
+            for q in [
+                m
+                for m in range(19)
+                if LATTICE_VECTORS[m][0] * sz >= dz - 1 and LATTICE_VECTORS[m][1] * sx >= dx - 1
+            ]
+            + extra
+        ]
+        for sz, sx in DIRECTIONS[4:]
+    ]
+
+
+RATE, DENSITY, MOMENTUM, CHANNELS = 19, 20, 21, 24
+MOVES = (slab_moves([]), cross_moves([]), corner_moves([]))
+EXTRA = list(range(19, CHANNELS))
+RAW_MOVES = (slab_moves(EXTRA), cross_moves(EXTRA), corner_moves(EXTRA))
+
+
+def buffer_shapes(moves, plane_count, columns, rows):
+    return [
+        (2, len(moves[0][0]), columns, rows),
+        (2, round_up(len(moves[1][0]) * plane_count, 8), rows),
+        (4, round_up(len(moves[2][0]), 8), rows),
+    ]
 
 
 def round_up(value, unit):
@@ -235,29 +270,35 @@
     return density, momentum
 
 
-def collide(fields, rate, pushed):
+def local_moments(fields):
+    gaps = [fields[q] - fields[q + 1] for q in range(1, 19, 2)]
     sums = [fields[q] + fields[q + 1] for q in range(1, 19, 2)]
-    gaps = [fields[q] - fields[q + 1] for q in range(1, 19, 2)]
     density = functools.reduce(lambda a, b: a + b, sums) + fields[0]
-    scale = 3.0 / density
-    tripled = []
+    momentum = []
     for k in range(3):
-        total = pushed[k]
+        total = None
         for pair in range(9):
             c = LATTICE_VECTORS[2 * pair + 1][k]
-            if c:
+            if c and total is None:
+                total = gaps[pair]
+            elif c:
                 total = total + gaps[pair] if c == 1 else total - gaps[pair]
-        tripled.append(total * scale)
+        momentum.append(total)
+    return density, momentum
+
+
+def pull_terms(density, momentum, rate, pushed, needed):
+    scale = 3.0 / density
+    tripled = [(m + p) * scale for m, p in zip(momentum, pushed)]
     squared = tripled[0] * tripled[0] + tripled[1] * tripled[1] + tripled[2] * tripled[2]
     base = 1.0 - (1.0 / 6.0) * squared
-    fluid = rate > 0.0
-    keep = 1.0 - rate
     strength = rate * density
     scaled = {w: w * strength for w in (1.0 / 18.0, 1.0 / 36.0)}
     result = [None] * 19
-    rest = keep * fields[0] + (LATTICE_WEIGHTS[0] * strength) * base
-    result[0] = jnp.where(fluid, rest, fields[0])
+    result[0] = (LATTICE_WEIGHTS[0] * strength) * base
     for q in range(1, 19, 2):
+        if q not in needed and q + 1 not in needed:
+            continue
         projected = None
         for c, v in zip(LATTICE_VECTORS[q], tripled):
             if c == 0:
@@ -269,9 +310,17 @@
         weight = scaled[LATTICE_WEIGHTS[q]]
         even = weight * (base + 0.5 * projected * projected)
         odd = weight * projected
-        result[q] = jnp.where(fluid, keep * fields[q] + (even + odd), fields[q + 1])
-        result[q + 1] = jnp.where(fluid, keep * fields[q + 1] + (even - odd), fields[q])
+        result[q] = even + odd
+        result[q + 1] = even - odd
     return result
+
+
+def collide(fields, rate, pushed, needed=range(19)):
+    density, momentum = local_moments(fields)
+    terms = pull_terms(density, momentum, rate, pushed, needed)
+    fluid = rate > 0.0
+    keep = 1.0 - rate
+    return {q: jnp.where(fluid, keep * fields[q] + terms[q], fields[OPPOSITE[q]]) for q in needed}
 
 
 def lattice_kernel(
@@ -282,7 +331,8 @@
     xs, inc, nodal, cell_ref, lane_ref, acc, along, across,
     raw, own_force, far_force, pushed, placed_ref, rim, post_one, post_two, post_three,
     coarse_all, table, faces,
-    zsend, zrecv, xsend, xrecv, csend, crecv,
+    zsend, xsend, csend, zrecv, xrecv, crecv,
+    raw_zsend, raw_xsend, raw_csend, raw_zrecv, raw_xrecv, raw_crecv,
     load_sems, coarse_sems, raw_sems, force_sems, face_sems, halo_sems,
 ):
     _, plane_count, columns, rows = pop_ref.shape
@@ -309,25 +359,64 @@
     def cubed(ref):
         return ref.reshape(ref.shape[0], wide + 2, extent, rows)
 
-    def spans(step, size, depth):
-        if step == 1:
-            return HALO + size - depth, HALO - depth, depth
-        if step == -1:
-            return HALO, HALO + size, depth
-        return HALO, HALO, size
-
-    def block_copy(ref, sems, index, depth):
-        dz, dx = DIRECTIONS[index]
-        z_from, z_to, z_size = spans(dz, plane_count, depth)
-        x_from, x_to, x_size = spans(dx, columns, depth)
-        whole = cubed(ref)
+    def inner_row(step, depth, size):
+        return HALO + (size - depth if step == 1 else depth - 1)
+
+    def outer_row(step, depth, size):
+        return HALO + (-depth if step == 1 else size - 1 + depth)
+
+    def pack(source, moves, buffers):
+        for side in range(4):
+            sz, sx = DIRECTIONS[4 + side]
+            for e, (q, dz, dx) in enumerate(moves[2][side]):
+                row = (inner_row(sx, dx, columns) + 1) * extent + inner_row(sz, dz, plane_count)
+                buffers[2][side, pl.ds(e, 1), :] = source[q, pl.ds(row, 1), :]
+        for side in range(2):
+            for e, (q, depth) in enumerate(moves[1][side]):
+                row = (inner_row(DIRECTIONS[2 + side][1], depth, columns) + 1) * extent + HALO
+                buffers[1][side, pl.ds(e * plane_count, plane_count), :] = source[
+                    q, pl.ds(row, plane_count), :
+                ]
+
+    def unpack(sink, moves, buffers):
+        for side in range(2):
+            for e, (q, depth) in enumerate(moves[0][side]):
+                row = outer_row(DIRECTIONS[side][0], depth, plane_count)
+                sink[q, plane_rows(row - HALO), :] = buffers[0][side, e]
+            for e, (q, depth) in enumerate(moves[1][side]):
+                row = (outer_row(DIRECTIONS[2 + side][1], depth, columns) + 1) * extent + HALO
+                sink[q, pl.ds(row, plane_count), :] = buffers[1][
+                    side, pl.ds(e * plane_count, plane_count), :
+                ]
+        for side in range(4):
+            sz, sx = DIRECTIONS[4 + side]
+            for e, (q, dz, dx) in enumerate(moves[2][side]):
+                row = (outer_row(sx, dx, columns) + 1) * extent + outer_row(sz, dz, plane_count)
+                sink[q, pl.ds(row, 1), :] = buffers[2][side, pl.ds(e, 1), :]
+
+    def keep_plane(q, p, value, moves, buffer):
+        for side in range(2):
+            entry = (q, plane_count - p if side == 0 else p + 1)
+            if entry in moves[0][side]:
+                buffer[side, moves[0][side].index(entry)] = value
+
+    def buffers_copy(sources, sinks, sems, index):
+        kind, place = (0, index) if index < 2 else (1, index - 2) if index < 4 else (2, index - 4)
         return pltpu.make_async_remote_copy(
-            src_ref=whole.at[:, pl.ds(1 + x_from, x_size), pl.ds(z_from, z_size)],
-            dst_ref=whole.at[:, pl.ds(1 + x_to, x_size), pl.ds(z_to, z_size)],
+            src_ref=sources[kind].at[place],
+            dst_ref=sinks[kind].at[place],
             send_sem=sems.at[0, index],
             recv_sem=sems.at[1, index],
             device_id=target(DIRECTIONS[index]),
             device_id_type=MESH,
+        )
+
+    def halo_copy(index):
+        return buffers_copy((zsend, xsend, csend), (zrecv, xrecv, crecv), halo_sems, index)
+
+    def raw_copy(index):
+        return buffers_copy(
+            (raw_zsend, raw_xsend, raw_csend), (raw_zrecv, raw_xrecv, raw_crecv), raw_sems, index
         )
 
     def column_rows(c):
@@ -377,46 +466,40 @@
             )
 
     def clear(side):
-        dz, dx = DIRECTIONS[side]
-        for c in range(-1, wide + 1):
-            if dx == 1 and c >= HALO or dx == -1 and c < HALO + columns:
-                continue
-            start = (c + 1) * extent
-            if dz == 1:
-                start, size = start, HALO
-            elif dz == -1:
-                start, size = start + HALO + plane_count, HALO
-            else:
-                size = extent
-            for q in range(20):
-                raw[q, pl.ds(start, size), :] = jnp.zeros((size, rows), F32)
-        if dx == 0:
-            zrecv[side] = jnp.zeros(zrecv.shape[1:], F32)
-            near = 0 if dz == 1 else extent // 2
+        kind, place = (0, side) if side < 2 else (1, side - 2) if side < 4 else (2, side - 4)
+        for sinks in ((zrecv, xrecv, crecv), (raw_zrecv, raw_xrecv, raw_crecv)):
+            sinks[kind][place] = jnp.zeros(sinks[kind].shape[1:], F32)
+        faces[side] = jnp.full(faces.shape[1:], -1, I32)
+        if side < 2:
+            near = side * (extent // 2)
             for c in range(wide):
                 for k in range(3):
                     far_force[k, pl.ds((c + 1) * extent + near, extent // 2), :] = jnp.zeros(
                         (extent // 2, rows), F32
                     )
-        else:
-            xrecv[side - 2] = jnp.zeros(xrecv.shape[1:], F32)
-
-    for side in range(4):
+
+    for side in range(8):
 
         @pl.when(jnp.logical_not(beside(DIRECTIONS[side], -1)))
         def _():
             clear(side)
-
-    for index in range(8):
-
-        @pl.when(jnp.logical_not(beside(DIRECTIONS[index], -1)))
-        def _():
-            faces[index] = jnp.full(faces.shape[1:], -1, I32)
-            if index >= 4:
-                crecv[index - 4] = jnp.zeros(crecv.shape[1:], F32)
 
     loads[0].wait()
     incidence_stage(tri_ref, inc, pos_ref.shape[2])
+    for load in loads[1:4]:
+        load.wait()
+    for p in range(plane_count):
+        at = plane_rows(p)
+        fields = [pop_ref[q, p] for q in range(19)]
+        density, momentum = local_moments(fields)
+        fluid = fluid_ref[p] == 1
+        keep = 1.0 - relax_ref[p]
+        values = [jnp.where(fluid, keep * fields[q], fields[OPPOSITE[q]]) for q in range(19)]
+        values += [jnp.where(fluid, relax_ref[p], 0.0), density] + momentum
+        for q, value in enumerate(values):
+            raw[q, at, :] = value
+            keep_plane(q, p, value, RAW_MOVES, raw_zsend)
+    pack(raw, RAW_MOVES, (None, raw_xsend, raw_csend))
     loads[6].wait()
     pl.semaphore_wait(barrier, expected)
 
@@ -454,17 +537,11 @@
         def _():
             face_copy(index).start()
 
-    for load in loads[1:4]:
-        load.wait()
-    for p in range(plane_count):
-        for q in range(19):
-            raw[q, plane_rows(p), :] = pop_ref[q, p]
-        raw[19, plane_rows(p), :] = jnp.where(fluid_ref[p] == 1, relax_ref[p], 0.0)
     for index in (4, 5, 6, 7, 0, 1, 2, 3):
 
         @pl.when(beside(DIRECTIONS[index], 1))
         def _():
-            block_copy(raw, raw_sems, index, HALO).start()
+            raw_copy(index).start()
 
     for load in loads[4:6]:
         load.wait()
@@ -641,7 +718,9 @@
 
         @pl.when(beside(DIRECTIONS[index], -1))
         def _():
-            block_copy(raw, raw_sems, index, HALO).wait_recv()
+            raw_copy(index).wait_recv()
+
+    unpack(raw, RAW_MOVES, (raw_zrecv, raw_xrecv, raw_crecv))
 
     def pulled(source, at, starts):
         fixed = placed_ref[4, at, :] > 0.5
@@ -663,9 +742,16 @@
     def pulled_plane(source, p):
         return pulled(source, plane_rows(p), lambda cz, cx: plane_rows(p, cz, cx))
 
+    def inward(c, depth):
+        if c < HALO:
+            return [q for q in range(19) if LATTICE_VECTORS[q][1] >= HALO - c - depth]
+        if c >= HALO + columns:
+            return [q for q in range(19) if -LATTICE_VECTORS[q][1] >= c - HALO - columns + 1 - depth]
+        return range(19)
+
     for c in range(wide):
         at = column_rows(c)
-        rate = raw[19, at, :]
+        rate = raw[RATE, at, :]
         fluid = rate > 0.0
         inverse = 1.0 / rate
         push = []
@@ -673,15 +759,19 @@
             value = jnp.where(fluid, (own_force[k, at, :] + far_force[k, at, :]) * inverse, 0.0)
             pushed[k, at, :] = value
             push.append(value)
-        for q, value in enumerate(collide([raw[q, at, :] for q in range(19)], rate, push)):
-            post_one[q, at, :] = value
+        momentum = [raw[MOMENTUM + k, at, :] for k in range(3)]
+        needed = inward(c, 1)
+        terms = pull_terms(raw[DENSITY, at, :], momentum, rate, push, needed)
+        for q in needed:
+            kept = raw[q, at, :]
+            post_one[q, at, :] = jnp.where(fluid, kept + terms[q], kept)
 
     def collide_columns(source, sink):
         for c in range(1, wide - 1):
             at = column_rows(c)
             fields = pulled_column(source, c)
             push = [pushed[k, at, :] for k in range(3)]
-            for q, value in enumerate(collide(fields, raw[19, at, :], push)):
+            for q, value in collide(fields, raw[RATE, at, :], push, inward(c, 0)).items():
                 sink[q, at, :] = value
 
     collide_columns(post_one, post_two)
@@ -690,46 +780,10 @@
         at = plane_rows(p)
         fields = pulled_plane(post_two, p)
         push = [pushed[k, at, :] for k in range(3)]
-        for q, value in enumerate(collide(fields, raw[19, at, :], push)):
+        for q, value in collide(fields, raw[RATE, at, :], push).items():
             post_three[q, at, :] = value
-            for side in range(2):
-                depth = plane_count - p if side == 0 else p + 1
-                if (q, depth) in SLAB_MOVES[side]:
-                    zsend[side, SLAB_MOVES[side].index((q, depth))] = value
-
-    def inner_row(step, depth, size):
-        return HALO + (size - depth if step == 1 else depth - 1)
-
-    def outer_row(step, depth, size):
-        return HALO + (-depth if step == 1 else size - 1 + depth)
-
-    for side in range(4):
-        for e, (q, dz, dx) in enumerate(CORNER_MOVES[side]):
-            sz, sx = DIRECTIONS[4 + side]
-            row = (inner_row(sx, dx, columns) + 1) * extent + inner_row(sz, dz, plane_count)
-            csend[side, pl.ds(e, 1), :] = post_three[q, pl.ds(row, 1), :]
-    for side in range(2):
-        for e, (q, depth) in enumerate(CROSS_MOVES[side]):
-            row = (inner_row(DIRECTIONS[2 + side][1], depth, columns) + 1) * extent + HALO
-            xsend[side, pl.ds(e * plane_count, plane_count), :] = post_three[
-                q, pl.ds(row, plane_count), :
-            ]
-
-    def halo_copy(index):
-        if index < 2:
-            source, sink = zsend.at[index], zrecv.at[index]
-        elif index < 4:
-            source, sink = xsend.at[index - 2], xrecv.at[index - 2]
-        else:
-            source, sink = csend.at[index - 4], crecv.at[index - 4]
-        return pltpu.make_async_remote_copy(
-            src_ref=source,
-            dst_ref=sink,
-            send_sem=halo_sems.at[0, index],
-            recv_sem=halo_sems.at[1, index],
-            device_id=target(DIRECTIONS[index]),
-            device_id_type=MESH,
-        )
+            keep_plane(q, p, value, MOVES, zsend)
+    pack(post_three, MOVES, (None, xsend, csend))
 
     for index in (4, 5, 6, 7, 0, 1, 2, 3):
 
@@ -743,21 +797,7 @@
         def _():
             halo_copy(index).wait_recv()
 
-    for side in range(2):
-        for e, (q, depth) in enumerate(SLAB_MOVES[side]):
-            row = outer_row(DIRECTIONS[side][0], depth, plane_count)
-            post_three[q, plane_rows(row - HALO), :] = zrecv[side, e]
-        for e, (q, depth) in enumerate(CROSS_MOVES[side]):
-            row = (outer_row(DIRECTIONS[2 + side][1], depth, columns) + 1) * extent + HALO
-            post_three[q, pl.ds(row, plane_count), :] = xrecv[
-                side, pl.ds(e * plane_count, plane_count), :
-            ]
-    for side in range(4):
-        for e, (q, dz, dx) in enumerate(CORNER_MOVES[side]):
-            sz, sx = DIRECTIONS[4 + side]
-            row = (outer_row(sx, dx, columns) + 1) * extent + outer_row(sz, dz, plane_count)
-            post_three[q, pl.ds(row, 1), :] = crecv[side, pl.ds(e, 1), :]
-
+    unpack(post_three, MOVES, (zrecv, xrecv, crecv))
     collide_columns(post_three, post_one)
 
     for p in range(plane_count):
@@ -772,7 +812,7 @@
 
         @pl.when(beside(DIRECTIONS[index], 1))
         def _():
-            block_copy(raw, raw_sems, index, HALO).wait_send()
+            raw_copy(index).wait_send()
             face_copy(index).wait_send()
             halo_copy(index).wait_send()
             if index < 2:
@@ -831,7 +871,7 @@
             pltpu.VMEM((6 * cells, 2 * rows), F32),
             pltpu.VMEM((3, half * planes + cells, rows), F32),
             pltpu.VMEM((3, (columns + 4) * planes + 16, rows), F32),
-            pltpu.VMEM((20, flat, rows), F32),
+            pltpu.VMEM((CHANNELS, flat, rows), F32),
             pltpu.VMEM((3, flat, rows), F32),
             pltpu.VMEM((3, flat, rows), F32),
             pltpu.VMEM((3, flat, rows), F32),
@@ -843,12 +883,13 @@
             pltpu.VMEM((slabs,) + coarse_moments.shape, F32),
             pltpu.VMEM((coarse_rows(slabs, coarse_moments), 128), F32),
             pltpu.VMEM((8,) + interface.shape, I32),
-            pltpu.VMEM((2, 19, columns, rows), F32),
-            pltpu.VMEM((2, 19, columns, rows), F32),
-            pltpu.VMEM((2, round_up(19 * plane_count, 8), rows), F32),
-            pltpu.VMEM((2, round_up(19 * plane_count, 8), rows), F32),
-            pltpu.VMEM((4, 24, rows), F32),
-            pltpu.VMEM((4, 24, rows), F32),
+        ]
+        + [
+            pltpu.VMEM(shape, F32)
+            for moves in (MOVES, MOVES, RAW_MOVES, RAW_MOVES)
+            for shape in buffer_shapes(moves, plane_count, columns, rows)
+        ]
+        + [
             pltpu.SemaphoreType.DMA((8,)),
             pltpu.SemaphoreType.DMA((2, slabs)),
             pltpu.SemaphoreType.DMA((2, 8)),

time: 20.3 us -> 18.4 us (0.906)
  Pallas kernels: 19.5 us -> 17.6 us
    pallas_call x1, Pallas kernels: 18.8 us -> 16.8 us  [on_device(): pl.pallas_call(functools.partial(lattice_kernel, slabs, crosses), name='l...]
where the time goes in v4:
time: 18.4 us; the launch traced here: 18.2 us
  Pallas kernels  17.6 us (96%)
  between operations  0.64 us (3%)
    pallas_call x1, Pallas kernels, on_device(): pl.pallas_call(functools.partial(lattice_kernel, slabs, crosses), name='l...  16.8 us
    pallas_call x1, Pallas kernels, on_device(): pl.pallas_call(flow_kernel, name='flow', out_shape=(jax.ShapeDtypeStruct(...  0.74 us

profile of v4, /device:TPU:11, one launch (start us, length us, event | category | flops | bytes accessed | tf_op | source)
XLA Modules:
  0.0 18.2 jit_solution(2344454084385152931)
XLA Ops:
  0.6 16.8 %lattice_steps.1.fields_ref = f32[19,4,8,128]{3,2,1,0:T(8,128)S(1)} custom-call(s32[3,1280]{1,0:T(4,128)} %tri_hbm.1, f32[19,4,8,128]{3,2,1,0:T(8,128)} %pop_hbm.1, f32[4,8,128]{2,1,0:T(8,128)} %relax_hbm.1, s32[4,8,128]{2,1,0:T(8,128)} %fluid_hbm.1, s32[3,16,642]{2,1,0:T(8,128)} %pos_hbm.1, f32[16,1280]{1,0:T(8,128)} %ten_hbm.1, f32[4,512]{1,0:T(4,128)} %coarse_hbm.1, ...), custom_call_target="tpu_custom_call" | custom-call | tf_op jit(solution)/shard_map/lattice_steps/pallas_call | solution.py:858
  17.5 0.7 %flow.1 = (f32[19,4,8,128]{3,2,1,0:T(8,128)}, f32[3,4,8,128]{3,2,1,0:T(8,128)}) custom-call(f32[19,4,8,128]{3,2,1,0:T(8,128)S(1)} %lattice_steps.1.fields_ref), custom_call_target="tpu_custom_call" | custom-call | tf_op jit(solution)/shard_map/flow/pallas_call | solution.py:902

commit v5 on v4

--- a/solution.py
+++ b/solution.py
@@ -117,14 +117,15 @@
         for k in range(3)
     ]
     iota = lax.broadcasted_iota(I32, (16, 128), 0)
+    zero, one = jnp.zeros((16, 128), BF16), jnp.ones((16, 128), BF16)
 
     def rows_at(start):
         ids = (iota + start).astype(I16)
         for t in range(tiles):
-            hit = (ids == corners[0][t]) | (ids == corners[1][t]) | (ids == corners[2][t])
-            inc[pl.ds(start, 16), t * 128 : (t + 1) * 128] = jnp.where(
-                hit, jnp.ones((), BF16), jnp.zeros((), BF16)
-            )
+            value = zero
+            for k in range(3):
+                value = jnp.where(ids == corners[k][t], one, value)
+            inc[pl.ds(start, 16), t * 128 : (t + 1) * 128] = value
 
     chunk = 128
 
@@ -178,37 +179,64 @@
         force[k] = total[k * membranes : (k + 1) * membranes] - 3.0 * xs[k] * weight
 
 
-def spread_stage(plane_count, columns, cell_ref, lane_ref, force, acc, along, across, out_ref):
+def spread_stage(plane_count, columns, nodes, cell_ref, lane_ref, force, acc, along, across, out_ref):
     _, membranes, padded = force.shape
     rows = out_ref.shape[2]
     planes, half = plane_count + 2, (columns + 6) // 2
     extent = plane_count + 2 * HALO
     cells = acc.shape[0] // 6
-    acc[...] = jnp.zeros_like(acc)
     unroll = 4 if membranes % 4 == 0 else 1
     zero, one = jnp.zeros((), BF16), jnp.ones((), BF16)
 
+    main = nodes // 128 * 128
+    tail = nodes - main
+    packed = 0 < tail * membranes <= 128
+    if not packed:
+        main = padded
+
+    def one_hots(cell, lane, force_rows):
+        mask = lax.broadcasted_iota(I16, (cells, cell.shape[1]), 0) == cell.astype(I16)
+        values = [split(value, 2) for value in force_rows]
+        left = jnp.concatenate(
+            [
+                jnp.where(mask, values[k][part].astype(BF16), zero)
+                for part in range(2)
+                for k in range(3)
+            ],
+            axis=0,
+        )
+        ids = lax.broadcasted_iota(I16, (2 * rows, cell.shape[1]), 0)
+        return left, jnp.where(ids == lane.astype(I16), one, zero)
+
+    def gathered_tail(value):
+        lanes = lax.broadcasted_iota(I32, (membranes, 128), 1)
+        value = jnp.where(lanes < tail, value, jnp.zeros_like(value))
+        value = pltpu.roll(value, 0, 1, stride=tail, stride_axis=0)
+        return jnp.sum(value, axis=0, keepdims=True)
+
+    if packed:
+        ends = slice(main, main + 128)
+        left, right = one_hots(
+            gathered_tail(cell_ref[:, ends] + 1) - 1,
+            gathered_tail(lane_ref[:, ends] + 1) - 1,
+            [gathered_tail(force[k, :, ends]) for k in range(3)],
+        )
+        acc[...] = lax.dot_general(left, right, NT, preferred_element_type=F32)
+    else:
+        acc[...] = jnp.zeros_like(acc)
+
     @pl.loop(0, membranes // unroll)
     def _(i):
-        running = None
+        parts = []
         for inner in range(unroll):
             m = pl.ds(i * unroll + inner, 1)
-            cell = cell_ref[m, :].astype(I16)
-            lane = lane_ref[m, :].astype(I16)
-            mask = lax.broadcasted_iota(I16, (cells, padded), 0) == cell
-            values = [split(force[k, m, :], 2) for k in range(3)]
-            left = jnp.concatenate(
-                [
-                    jnp.where(mask, values[k][part].astype(BF16), zero)
-                    for part in range(2)
-                    for k in range(3)
-                ],
-                axis=0,
+            parts.append(
+                one_hots(
+                    cell_ref[m, :main], lane_ref[m, :main], [force[k, m, :main] for k in range(3)]
+                )
             )
-            right = jnp.where(lax.broadcasted_iota(I16, (2 * rows, padded), 0) == lane, one, zero)
-            product = lax.dot_general(left, right, NT, preferred_element_type=F32)
-            running = product if running is None else running + product
-        acc[...] += running
+        left, right = (jnp.concatenate(side, axis=1) for side in zip(*parts))
+        acc[...] += lax.dot_general(left, right, NT, preferred_element_type=F32)
 
     used = half * planes
     inner = (columns + 4) * planes
@@ -365,16 +393,18 @@
     def outer_row(step, depth, size):
         return HALO + (-depth if step == 1 else size - 1 + depth)
 
-    def pack(source, moves, buffers):
+    def pack_corners(source, moves, buffer):
         for side in range(4):
             sz, sx = DIRECTIONS[4 + side]
             for e, (q, dz, dx) in enumerate(moves[2][side]):
                 row = (inner_row(sx, dx, columns) + 1) * extent + inner_row(sz, dz, plane_count)
-                buffers[2][side, pl.ds(e, 1), :] = source[q, pl.ds(row, 1), :]
+                buffer[side, pl.ds(e, 1), :] = source[q, pl.ds(row, 1), :]
+
+    def pack_cross(source, moves, buffer):
         for side in range(2):
             for e, (q, depth) in enumerate(moves[1][side]):
                 row = (inner_row(DIRECTIONS[2 + side][1], depth, columns) + 1) * extent + HALO
-                buffers[1][side, pl.ds(e * plane_count, plane_count), :] = source[
+                buffer[side, pl.ds(e * plane_count, plane_count), :] = source[
                     q, pl.ds(row, plane_count), :
                 ]
 
@@ -499,25 +529,44 @@
         for q, value in enumerate(values):
             raw[q, at, :] = value
             keep_plane(q, p, value, RAW_MOVES, raw_zsend)
-    pack(raw, RAW_MOVES, (None, raw_xsend, raw_csend))
+    pack_corners(raw, RAW_MOVES, raw_csend)
+    pack_cross(raw, RAW_MOVES, raw_xsend)
     loads[6].wait()
     pl.semaphore_wait(barrier, expected)
 
-    coarse_all[slab] = coarse_ref[...]
-
-    def coarse_copy(d):
+    ways = 2 if slabs % 2 == 0 else 1
+    share = slabs // ways
+    way = slab % ways
+
+    def place_of(index):
+        return index % ways * share + index // ways
+
+    coarse_all[place_of(slab)] = coarse_ref[...]
+
+    def coarse_copy(d, sink):
         return pltpu.make_async_remote_copy(
             src_ref=coarse_ref,
-            dst_ref=coarse_all.at[slab],
+            dst_ref=coarse_all.at[place_of(sink)],
             send_sem=coarse_sems.at[0, d],
             recv_sem=coarse_sems.at[1, d],
-            device_id={"slab": lax.rem(slab + d, slabs), "cross": cross},
+            device_id={"slab": lax.rem(slab + ways * d, slabs), "cross": cross},
             device_id_type=MESH,
         )
 
-    @pl.loop(1, slabs)
+    def relay():
+        half = coarse_all.at[pl.ds(way * share, share)]
+        return pltpu.make_async_remote_copy(
+            src_ref=half,
+            dst_ref=half,
+            send_sem=coarse_sems.at[0, 0],
+            recv_sem=coarse_sems.at[1, 0],
+            device_id={"slab": slab + 1 - 2 * way, "cross": cross},
+            device_id_type=MESH,
+        )
+
+    @pl.loop(1, share)
     def _(d):
-        coarse_copy(d).start()
+        coarse_copy(d, slab).start()
 
     loads[7].wait()
 
@@ -548,7 +597,7 @@
     nodal_stage(
         plane_count, columns, rows, pos_ref, ten_ref, inc, xs, cell_ref, lane_ref, nodal
     )
-    spread_stage(plane_count, columns, cell_ref, lane_ref, nodal, acc, along, across, own_force)
+    spread_stage(plane_count, columns, pos_ref.shape[2], cell_ref, lane_ref, nodal, acc, along, across, own_force)
 
     def force_copy(index):
         part = extent // 2
@@ -568,14 +617,18 @@
         def _():
             force_copy(index).start()
 
-    @pl.loop(1, slabs)
+    @pl.loop(1, share)
     def _(d):
+        coarse_copy(d, lax.rem(slab + slabs - ways * d, slabs)).wait_recv()
+
+    if ways == 2:
+        relay().start()
         pltpu.make_async_remote_copy(
-            src_ref=coarse_ref,
-            dst_ref=coarse_all.at[lax.rem(slab + slabs - d, slabs)],
-            send_sem=coarse_sems.at[0, d],
-            recv_sem=coarse_sems.at[1, d],
-            device_id={"slab": lax.rem(slab + d, slabs), "cross": cross},
+            src_ref=coarse_all.at[pl.ds(way * share, share)],
+            dst_ref=coarse_all.at[pl.ds((1 - way) * share, share)],
+            send_sem=coarse_sems.at[0, 0],
+            recv_sem=coarse_sems.at[1, 0],
+            device_id={"slab": slab + 1 - 2 * way, "cross": cross},
             device_id_type=MESH,
         ).wait_recv()
 
@@ -609,7 +662,7 @@
         for j in range(together):
             for chunk in range(chunks):
                 table[pl.ds((j * chunks + chunk) * 4, 4), :] = coarse_all[
-                    base * together + j, :, chunk * lanes : (chunk + 1) * lanes
+                    place_of(base * together + j), :, chunk * lanes : (chunk + 1) * lanes
                 ]
         stacked = jnp.concatenate(split(table[...], 2), axis=0).astype(BF16)
         result = []
@@ -708,19 +761,19 @@
         for q, value in enumerate(equilibrium_pairs(density, velocity)):
             rim[q, at, :] = value
 
+    for index in range(8):
+
+        @pl.when(beside(DIRECTIONS[index], -1))
+        def _():
+            raw_copy(index).wait_recv()
+
+    unpack(raw, RAW_MOVES, (raw_zrecv, raw_xrecv, raw_crecv))
+
     for index in range(2):
 
         @pl.when(beside(DIRECTIONS[index], -1))
         def _():
             force_copy(index).wait_recv()
-
-    for index in range(8):
-
-        @pl.when(beside(DIRECTIONS[index], -1))
-        def _():
-            raw_copy(index).wait_recv()
-
-    unpack(raw, RAW_MOVES, (raw_zrecv, raw_xrecv, raw_crecv))
 
     def pulled(source, at, starts):
         fixed = placed_ref[4, at, :] > 0.5
@@ -776,6 +829,13 @@
 
     collide_columns(post_one, post_two)
 
+    def send_halo(indices):
+        for index in indices:
+
+            @pl.when(beside(DIRECTIONS[index], 1))
+            def _():
+                halo_copy(index).start()
+
     for p in range(plane_count):
         at = plane_rows(p)
         fields = pulled_plane(post_two, p)
@@ -783,19 +843,41 @@
         for q, value in collide(fields, raw[RATE, at, :], push).items():
             post_three[q, at, :] = value
             keep_plane(q, p, value, MOVES, zsend)
-    pack(post_three, MOVES, (None, xsend, csend))
-
-    for index in (4, 5, 6, 7, 0, 1, 2, 3):
+        if p == HALO - 1:
+            send_halo([1])
+    send_halo([0])
+    pack_corners(post_three, MOVES, csend)
+    send_halo([4, 5, 6, 7])
+    pack_cross(post_three, MOVES, xsend)
+    send_halo([2, 3])
+
+    @pl.loop(1, share)
+    def _(d):
+        coarse_copy(d, slab).wait_send()
+
+    if ways == 2:
+        relay().wait_send()
+
+    for index in range(8):
 
         @pl.when(beside(DIRECTIONS[index], 1))
         def _():
-            halo_copy(index).start()
+            raw_copy(index).wait_send()
+            face_copy(index).wait_send()
+            if index < 2:
+                force_copy(index).wait_send()
 
     for index in range(8):
 
         @pl.when(beside(DIRECTIONS[index], -1))
         def _():
             halo_copy(index).wait_recv()
+
+    for index in range(8):
+
+        @pl.when(beside(DIRECTIONS[index], 1))
+        def _():
+            halo_copy(index).wait_send()
 
     unpack(post_three, MOVES, (zrecv, xrecv, crecv))
     collide_columns(post_three, post_one)
@@ -803,20 +885,6 @@
     for p in range(plane_count):
         for q, value in enumerate(pulled_plane(post_one, p)):
             next_ref[q, p] = value
-
-    @pl.loop(1, slabs)
-    def _(d):
-        coarse_copy(d).wait_send()
-
-    for index in range(8):
-
-        @pl.when(beside(DIRECTIONS[index], 1))
-        def _():
-            raw_copy(index).wait_send()
-            face_copy(index).wait_send()
-            halo_copy(index).wait_send()
-            if index < 2:
-                force_copy(index).wait_send()
 
 
 def flow_kernel(fields_ref, next_ref, flow_ref, flow, sems):

time: 18.4 us -> 18 us (0.978)
  Pallas kernels: 17.6 us -> 17.2 us
    pallas_call x1, Pallas kernels: 16.8 us -> 16.5 us  [on_device(): pl.pallas_call(functools.partial(lattice_kernel, slabs, crosses), name='l...]
where the time goes in v5:
time: 18 us; the launch traced here: 17.9 us
  Pallas kernels  17.2 us (96%)
  between operations  0.64 us (4%)
    pallas_call x1, Pallas kernels, on_device(): pl.pallas_call(functools.partial(lattice_kernel, slabs, crosses), name='l...  16.5 us
    pallas_call x1, Pallas kernels, on_device(): pl.pallas_call(flow_kernel, name='flow', out_shape=(jax.ShapeDtypeStruct(...  0.74 us

profile of v5, /device:TPU:11, one launch (start us, length us, event | category | flops | bytes accessed | tf_op | source)
XLA Modules:
  0.0 17.9 jit_solution(11005143966031606219)
XLA Ops:
  0.6 16.5 %lattice_steps.1.fields_ref = f32[19,4,8,128]{3,2,1,0:T(8,128)S(1)} custom-call(s32[3,1280]{1,0:T(4,128)} %tri_hbm.1, f32[19,4,8,128]{3,2,1,0:T(8,128)} %pop_hbm.1, f32[4,8,128]{2,1,0:T(8,128)} %relax_hbm.1, s32[4,8,128]{2,1,0:T(8,128)} %fluid_hbm.1, s32[3,16,642]{2,1,0:T(8,128)} %pos_hbm.1, f32[16,1280]{1,0:T(8,128)} %ten_hbm.1, f32[4,512]{1,0:T(4,128)} %coarse_hbm.1, ...), custom_call_target="tpu_custom_call" | custom-call | tf_op jit(solution)/shard_map/lattice_steps/pallas_call | solution.py:926
  17.1 0.7 %flow.1 = (f32[19,4,8,128]{3,2,1,0:T(8,128)}, f32[3,4,8,128]{3,2,1,0:T(8,128)}) custom-call(f32[19,4,8,128]{3,2,1,0:T(8,128)S(1)} %lattice_steps.1.fields_ref), custom_call_target="tpu_custom_call" | custom-call | tf_op jit(solution)/shard_map/flow/pallas_call | solution.py:970

commit v6 on v5

--- a/solution.py
+++ b/solution.py
@@ -179,7 +179,7 @@
         force[k] = total[k * membranes : (k + 1) * membranes] - 3.0 * xs[k] * weight
 
 
-def spread_stage(plane_count, columns, nodes, cell_ref, lane_ref, force, acc, along, across, out_ref):
+def spread_stage(plane_count, columns, nodes, cell_ref, lane_ref, force, acc, along, across, out_ref, ready):
     _, membranes, padded = force.shape
     rows = out_ref.shape[2]
     planes, half = plane_count + 2, (columns + 6) // 2
@@ -263,6 +263,7 @@
                 + weights[1] * across[k, start - 1 : start - 1 + extent]
                 + weights[2] * across[k, start : start + extent]
             )
+        ready(k)
 
 
 def equilibrium_pairs(density, velocity):
@@ -597,25 +598,29 @@
     nodal_stage(
         plane_count, columns, rows, pos_ref, ten_ref, inc, xs, cell_ref, lane_ref, nodal
     )
-    spread_stage(plane_count, columns, pos_ref.shape[2], cell_ref, lane_ref, nodal, acc, along, across, own_force)
-
-    def force_copy(index):
+    def force_copy(index, k):
         part = extent // 2
         start = part if index == 0 else 0
         return pltpu.make_async_remote_copy(
-            src_ref=cubed(own_force).at[:, pl.ds(1, wide), pl.ds(start, part)],
-            dst_ref=cubed(far_force).at[:, pl.ds(1, wide), pl.ds(part - start, part)],
-            send_sem=force_sems.at[0, index],
-            recv_sem=force_sems.at[1, index],
+            src_ref=cubed(own_force).at[pl.ds(k, 1), pl.ds(1, wide), pl.ds(start, part)],
+            dst_ref=cubed(far_force).at[pl.ds(k, 1), pl.ds(1, wide), pl.ds(part - start, part)],
+            send_sem=force_sems.at[0, 3 * index + k],
+            recv_sem=force_sems.at[1, 3 * index + k],
             device_id=target(DIRECTIONS[index]),
             device_id_type=MESH,
         )
 
-    for index in range(2):
-
-        @pl.when(beside(DIRECTIONS[index], 1))
-        def _():
-            force_copy(index).start()
+    def send_force(k):
+        for index in range(2):
+
+            @pl.when(beside(DIRECTIONS[index], 1))
+            def _():
+                force_copy(index, k).start()
+
+    spread_stage(
+        plane_count, columns, pos_ref.shape[2], cell_ref, lane_ref, nodal, acc, along, across, own_force,
+        send_force,
+    )
 
     @pl.loop(1, share)
     def _(d):
@@ -773,7 +778,8 @@
 
         @pl.when(beside(DIRECTIONS[index], -1))
         def _():
-            force_copy(index).wait_recv()
+            for k in range(3):
+                force_copy(index, k).wait_recv()
 
     def pulled(source, at, starts):
         fixed = placed_ref[4, at, :] > 0.5
@@ -865,7 +871,8 @@
             raw_copy(index).wait_send()
             face_copy(index).wait_send()
             if index < 2:
-                force_copy(index).wait_send()
+                for k in range(3):
+                    force_copy(index, k).wait_send()
 
     for index in range(8):
 
@@ -961,7 +968,7 @@
             pltpu.SemaphoreType.DMA((8,)),
             pltpu.SemaphoreType.DMA((2, slabs)),
             pltpu.SemaphoreType.DMA((2, 8)),
-            pltpu.SemaphoreType.DMA((2, 2)),
+            pltpu.SemaphoreType.DMA((2, 6)),
             pltpu.SemaphoreType.DMA((2, 8)),
             pltpu.SemaphoreType.DMA((2, 8)),
         ],

time: 18 us -> 18 us (level)
  no operation moved by 1% of the time
where the time goes in v6:
time: 18 us; the launch traced here: 17.9 us
  Pallas kernels  17.3 us (96%)
  between operations  0.64 us (4%)
    pallas_call x1, Pallas kernels, on_device(): pl.pallas_call(functools.partial(lattice_kernel, slabs, crosses), name='l...  16.5 us
    pallas_call x1, Pallas kernels, on_device(): pl.pallas_call(flow_kernel, name='flow', out_shape=(jax.ShapeDtypeStruct(...  0.74 us

profile of v6, /device:TPU:11, one launch (start us, length us, event | category | flops | bytes accessed | tf_op | source)
XLA Modules:
  0.0 17.9 jit_solution(17299054855399886142)
XLA Ops:
  0.6 16.5 %lattice_steps.1.fields_ref = f32[19,4,8,128]{3,2,1,0:T(8,128)S(1)} custom-call(s32[3,1280]{1,0:T(4,128)} %tri_hbm.1, f32[19,4,8,128]{3,2,1,0:T(8,128)} %pop_hbm.1, f32[4,8,128]{2,1,0:T(8,128)} %relax_hbm.1, s32[4,8,128]{2,1,0:T(8,128)} %fluid_hbm.1, s32[3,16,642]{2,1,0:T(8,128)} %pos_hbm.1, f32[16,1280]{1,0:T(8,128)} %ten_hbm.1, f32[4,512]{1,0:T(4,128)} %coarse_hbm.1, ...), custom_call_target="tpu_custom_call" | custom-call | tf_op jit(solution)/shard_map/lattice_steps/pallas_call | solution.py:933
  17.2 0.7 %flow.1 = (f32[19,4,8,128]{3,2,1,0:T(8,128)}, f32[3,4,8,128]{3,2,1,0:T(8,128)}) custom-call(f32[19,4,8,128]{3,2,1,0:T(8,128)S(1)} %lattice_steps.1.fields_ref), custom_call_target="tpu_custom_call" | custom-call | tf_op jit(solution)/shard_map/flow/pallas_call | solution.py:977
